TPU v7x, 32 devices: a whole 2x2x4 slice. The times are simulated.
32 devices in a mesh: fsdp: 4 (over z), ctx: 4 (over x, core), tp: 2 (over y).
Axes of the slice: x: 2, y: 2, z: 4, core: 2. Of those that a mesh axis runs over, the one named last changes fastest.
Arguments:
- hidden_in: bfloat16 [4, 2048, 2048], P('fsdp', 'ctx'), may hold values from -6 to 6
- out_grad: bfloat16 [4, 2048, 2048], P('fsdp', 'ctx'), may hold values from -6 to 6
- segment_ids: int32 [4, 2048], P('fsdp', 'ctx'), may hold values from 0 to 3, never falling along the last dimension, each value on 1 to 1024 neighbouring positions
- attn_gain: bfloat16 [2048], P('fsdp'), may hold values from 0.5 to 1.5
- w_query: bfloat16 [2048, 2048], P('fsdp', 'tp'), may hold values from -0.125 to 0.125
- w_key: bfloat16 [2048, 2048], P('fsdp', 'tp'), may hold values from -0.125 to 0.125
- w_value: bfloat16 [2048, 2048], P('fsdp', 'tp'), may hold values from -0.125 to 0.125
- w_out: bfloat16 [2048, 2048], P('tp', 'fsdp'), may hold values from -1 to 1
- mlp_gain: bfloat16 [2048], P('fsdp'), may hold values from 0.5 to 1.5
- w_gate: bfloat16 [2048, 8192], P('fsdp', 'tp'), may hold values from -0.125 to 0.125
- w_up: bfloat16 [2048, 8192], P('fsdp', 'tp'), may hold values from -0.125 to 0.125
- w_down: bfloat16 [8192, 2048], P('tp', 'fsdp'), may hold values from -0.0625 to 0.0625
Outputs:
- output: bfloat16 [4, 2048, 2048], P('fsdp', 'ctx')
- input_grad: bfloat16 [4, 2048, 2048], P('fsdp', 'ctx')
- attn_gain_grad: float32 [2048], P('fsdp')
- query_grad: float32 [2048, 2048], P('fsdp', 'tp')
- key_grad: float32 [2048, 2048], P('fsdp', 'tp')
- value_grad: float32 [2048, 2048], P('fsdp', 'tp')
- out_proj_grad: float32 [2048, 2048], P('tp', 'fsdp')
- mlp_gain_grad: float32 [2048], P('fsdp')
- gate_grad: float32 [2048, 8192], P('fsdp', 'tp')
- up_grad: float32 [2048, 8192], P('fsdp', 'tp')
- down_grad: float32 [8192, 2048], P('tp', 'fsdp')
Inputs may be any that keep to these rules, and one draw needn't show every extreme that they name: `segment_ids`: along each sequence the document numbers never fall; a document is a run of 1 to 1024 tokens of one number.
All inputs are finite; a program needn't handle non-finite values.
Results may differ from a plain program's by a relative error of at most 0.024.
Values may be sent and summed in bfloat16 or wider, within the bound.
A program may use at most 384 MiB of HBM per device.

v0:
```python
import math

import jax
import jax.numpy as jnp
from jax import lax
from jax.experimental import pallas as pl
from jax.experimental.pallas import tpu as pltpu
from jax.sharding import PartitionSpec as P


HEAD_DIM = 64
EPS = 1e-05
ROPE_BASE = 130000.0
MASKED = -1e30
PAIR = 2 * HEAD_DIM
BLOCK = 512
VMEM_LIMIT = 60 * 1024 * 1024


def low(values):
    return values.astype(jnp.bfloat16)


def wide(values):
    return values.astype(jnp.float32)


def product(a, b):
    return jnp.dot(a, b, preferred_element_type=jnp.float32)


def contract_rows(a, b):
    return lax.dot_general(a, b, (((0,), (0,)), ((), ())), preferred_element_type=jnp.float32)


def contract_cols(a, b):
    return lax.dot_general(a, b, (((1,), (1,)), ((), ())), preferred_element_type=jnp.float32)


def aligned(start, count):
    return pl.ds(pl.multiple_of(start, count), count)


def first_head():
    return lax.broadcasted_iota(jnp.int32, (1, PAIR), 1) < HEAD_DIM


def split_heads(rows):
    zero = jnp.zeros_like(rows)
    mask = first_head()
    return jnp.where(mask, rows, zero), jnp.where(mask, zero, rows)


def turn(rows, sign):
    half = HEAD_DIM // 2
    lanes = lax.broadcasted_iota(jnp.int32, (1, PAIR), 1)
    up = pltpu.roll(rows, PAIR - half, 1)
    down = pltpu.roll(rows, half, 1)
    return jnp.where(lanes % HEAD_DIM < half, -sign * up, sign * down)


def forward_kernel(info, qkv_ref, cos_ref, sin_ref, seg_col, seg_row, rot_ref, out_ref, wide_ref, lse_ref, best, total, acc):
    blocks = qkv_ref.shape[0] // BLOCK

    def prepare(n, _):
        rows = pl.ds(pl.multiple_of(n * BLOCK, BLOCK), BLOCK)
        cos, sin = cos_ref[rows, :], sin_ref[rows, :]
        q = qkv_ref[rows, :PAIR]
        k = qkv_ref[rows, PAIR : 2 * PAIR]
        rot_ref[rows, :PAIR] = low(low(q * cos + turn(q, 1.0) * sin) * jnp.bfloat16(HEAD_DIM**-0.5))
        rot_ref[rows, PAIR : 2 * PAIR] = low(k * cos + turn(k, 1.0) * sin)
        rot_ref[rows, 2 * PAIR :] = low(qkv_ref[rows, 2 * PAIR :])
        return 0

    lax.fori_loop(0, blocks, prepare, 0)

    def visit(i, j, diagonal):
        rows = pl.ds(pl.multiple_of(i * BLOCK, BLOCK), BLOCK)
        cols = pl.ds(pl.multiple_of(j * BLOCK, BLOCK), BLOCK)
        allowed = seg_col[rows, :1] == seg_row[:1, cols]
        if diagonal:
            at = lax.broadcasted_iota(jnp.int32, (BLOCK, BLOCK), 0)
            allowed = allowed & (at >= lax.broadcasted_iota(jnp.int32, (BLOCK, BLOCK), 1))
        keys = rot_ref[cols, PAIR : 2 * PAIR]
        values = rot_ref[cols, 2 * PAIR :]
        for h, q in enumerate(split_heads(rot_ref[rows, :PAIR])):
            scores = jnp.where(allowed, contract_cols(q, keys), MASKED)
            top = jnp.max(scores, axis=1, keepdims=True)
            if diagonal:
                p = jnp.exp(scores - top)
                best[h] = jnp.broadcast_to(top, (BLOCK, PAIR))
                total[h] = jnp.broadcast_to(jnp.sum(p, axis=1, keepdims=True), (BLOCK, PAIR))
                acc[h] = product(low(p), values)
            else:
                old = best[h][:, :1]
                new = jnp.maximum(old, top)
                fade = jnp.exp(old - new)
                p = jnp.exp(scores - new)
                best[h] = jnp.broadcast_to(new, (BLOCK, PAIR))
                total[h] = total[h] * fade + jnp.sum(p, axis=1, keepdims=True)
                acc[h] = acc[h] * fade + product(low(p), values)

    def one_row(i, _):
        rows = pl.ds(pl.multiple_of(i * BLOCK, BLOCK), BLOCK)
        visit(i, i, True)

        def one_col(j, _):
            @pl.when((info[0, j] < info[0, i]) & (info[2, j] >= info[1, i]))
            def _():
                visit(i, j, False)

            return 0

        lax.fori_loop(0, blocks, one_col, 0)
        mixed = jnp.where(first_head(), acc[0] / total[0], acc[1] / total[1])
        out_ref[rows, :] = low(mixed)
        wide_ref[rows, :] = mixed
        for h in range(2):
            lse_ref[0, h : h + 1, rows] = (best[h] + jnp.log(total[h])).T[:1, :]
        return 0

    lax.fori_loop(0, blocks, one_row, 0)


class Backward:
    def __init__(self, pair, rot, cos, sin, seg_col, seg_row, cot, mixed, lse, out, delta, dq, follows):
        self.pair, self.follows = pair, follows
        self.rot, self.cos, self.sin, self.seg_col, self.seg_row = rot, cos, sin, seg_col, seg_row
        self.cot, self.mixed, self.lse, self.out, self.delta, self.dq = cot, mixed, lse, out, delta, dq
        self.blocks = rot.shape[0] // BLOCK

    def part(self, n):
        return aligned((3 * self.pair + n) * PAIR, PAIR)

    def own(self):
        return aligned(self.pair * PAIR, PAIR)

    def prepare(self):
        def some(n, _):
            rows = aligned(n * BLOCK, BLOCK)
            terms = (wide(self.cot[rows, self.own()]) * self.mixed[rows, self.own()]).T
            self.delta[0:1, rows] = jnp.sum(terms[:HEAD_DIM], axis=0, keepdims=True)
            self.delta[1:2, rows] = jnp.sum(terms[HEAD_DIM:], axis=0, keepdims=True)
            self.dq[rows, :] = jnp.zeros((BLOCK, PAIR), jnp.float32)
            return 0

        lax.fori_loop(0, self.blocks, some, 0)

    def visit(self, row, rows_count, col, cols_count, diagonal, dk, dv):
        rows, cols = aligned(row, rows_count), aligned(col, cols_count)
        allowed = self.seg_col[cols, :1] == self.seg_row[:1, rows]
        if diagonal:
            at = lax.broadcasted_iota(jnp.int32, (cols_count, rows_count), 0)
            allowed = allowed & (at <= lax.broadcasted_iota(jnp.int32, (cols_count, rows_count), 1))
        queries, cots = self.rot[rows, self.part(0)], self.cot[rows, self.own()]
        query_heads, cot_heads = split_heads(queries), split_heads(cots)
        key_heads = split_heads(self.rot[cols, self.part(1)])
        value_heads = split_heads(self.rot[cols, self.part(2)])
        total = self.dq[rows, :]
        for h in range(2):
            scores = contract_cols(key_heads[h], queries)
            probs = jnp.where(allowed, jnp.exp(scores - self.lse[self.pair, h : h + 1, rows]), 0.0)
            dv = dv + product(low(probs), cot_heads[h])
            prob_cot = contract_cols(value_heads[h], cots)
            score_cot = low(probs * (prob_cot - self.delta[h : h + 1, rows]))
            dk = dk + product(score_cot, query_heads[h])
            total = total + contract_rows(score_cot, key_heads[h])
        self.dq[rows, :] = total
        return dk, dv

    def unturn(self, grad, rows):
        return low(grad * self.cos[rows, :] + turn(grad * self.sin[rows, :], -1.0))

    def column(self, j):
        start, half = j * BLOCK, BLOCK // 2
        zero = jnp.zeros((half, PAIR), jnp.float32)
        halves = [
            self.visit(start, BLOCK, start, half, True, zero, zero),
            self.visit(start + half, half, start + half, half, True, zero, zero),
        ]
        state = tuple(jnp.concatenate(pair, axis=0) for pair in zip(*halves))

        def one_row(i, state):
            return lax.cond(
                self.follows(i, j),
                lambda state: self.visit(i * BLOCK, BLOCK, start, BLOCK, False, *state),
                lambda state: state,
                state,
            )

        dk, dv = lax.fori_loop(0, self.blocks, one_row, state)
        cols = aligned(start, BLOCK)
        self.out[cols, self.part(1)] = self.unturn(dk, cols)
        self.out[cols, self.part(2)] = low(dv)

    def finish(self):
        def some(n, _):
            rows = aligned(n * BLOCK, BLOCK)
            self.out[rows, self.part(0)] = self.unturn(self.dq[rows, :] * HEAD_DIM**-0.5, rows)
            return 0

        lax.fori_loop(0, self.blocks, some, 0)


def backward_kernel(info, *refs):
    def follows(i, j):
        return (info[0, j] < info[0, i]) & (info[2, j] >= info[1, i])

    back = Backward(0, *refs, follows)
    back.prepare()

    def one_col(j, _):
        back.column(j)
        return 0

    lax.fori_loop(0, back.blocks, one_col, 0)
    back.finish()


def attention_forward(info, qkv, cos, sin, seg_col, seg_row):
    tokens, width = qkv.shape
    pairs = width // (3 * PAIR)
    whole = lambda p, info: (0, 0)
    return pl.pallas_call(
        forward_kernel,
        grid_spec=pltpu.PrefetchScalarGridSpec(
            num_scalar_prefetch=1,
            grid=(pairs,),
            in_specs=[
                pl.BlockSpec((tokens, 3 * PAIR), lambda p, info: (0, p)),
                pl.BlockSpec((tokens, PAIR), whole),
                pl.BlockSpec((tokens, PAIR), whole),
                pl.BlockSpec((tokens, 1), whole),
                pl.BlockSpec((1, tokens), whole),
            ],
            out_specs=[
                pl.BlockSpec((tokens, 3 * PAIR), lambda p, info: (0, p)),
                pl.BlockSpec((tokens, PAIR), lambda p, info: (0, p)),
                pl.BlockSpec((tokens, PAIR), lambda p, info: (0, p)),
                pl.BlockSpec((1, 2, tokens), lambda p, info: (p, 0, 0)),
            ],
            scratch_shapes=[
                pltpu.VMEM((2, BLOCK, PAIR), jnp.float32),
                pltpu.VMEM((2, BLOCK, PAIR), jnp.float32),
                pltpu.VMEM((2, BLOCK, PAIR), jnp.float32),
            ],
        ),
        out_shape=[
            jax.ShapeDtypeStruct((tokens, width), jnp.bfloat16),
            jax.ShapeDtypeStruct((tokens, pairs * PAIR), jnp.bfloat16),
            jax.ShapeDtypeStruct((tokens, pairs * PAIR), jnp.float32),
            jax.ShapeDtypeStruct((pairs, 2, tokens), jnp.float32),
        ],
        compiler_params=pltpu.CompilerParams(vmem_limit_bytes=VMEM_LIMIT),
        cost_estimate=pl.CostEstimate(flops=tokens * tokens * width, bytes_accessed=10 * tokens * width, transcendentals=tokens * tokens * 2 * pairs),
    )(info, qkv, cos, sin, seg_col, seg_row)


def attention_backward(info, rot, cos, sin, seg_col, seg_row, cot, mixed, lse):
    tokens, width = rot.shape
    pairs = width // (3 * PAIR)
    whole = lambda p, info: (0, 0)
    return pl.pallas_call(
        backward_kernel,
        grid_spec=pltpu.PrefetchScalarGridSpec(
            num_scalar_prefetch=1,
            grid=(pairs,),
            in_specs=[
                pl.BlockSpec((tokens, 3 * PAIR), lambda p, info: (0, p)),
                pl.BlockSpec((tokens, PAIR), whole),
                pl.BlockSpec((tokens, PAIR), whole),
                pl.BlockSpec((tokens, 1), whole),
                pl.BlockSpec((1, tokens), whole),
                pl.BlockSpec((tokens, PAIR), lambda p, info: (0, p)),
                pl.BlockSpec((tokens, PAIR), lambda p, info: (0, p)),
                pl.BlockSpec((1, 2, tokens), lambda p, info: (p, 0, 0)),
            ],
            out_specs=pl.BlockSpec((tokens, 3 * PAIR), lambda p, info: (0, p)),
            scratch_shapes=[
                pltpu.VMEM((2, tokens), jnp.float32),
                pltpu.VMEM((tokens, PAIR), jnp.float32),
            ],
        ),
        out_shape=jax.ShapeDtypeStruct((tokens, width), jnp.bfloat16),
        compiler_params=pltpu.CompilerParams(vmem_limit_bytes=VMEM_LIMIT),
        cost_estimate=pl.CostEstimate(flops=3 * tokens * tokens * width, bytes_accessed=10 * tokens * width, transcendentals=tokens * tokens * 2 * pairs),
    )(info, rot, cos, sin, seg_col, seg_row, cot, mixed, lse)


def swap(values, axis, mask):
    size = lax.axis_size(axis)
    return lax.ppermute(values, axis, [(i, i ^ mask) for i in range(size)])


def masks(size):
    return [1 << n for n in reversed(range(size.bit_length() - 1))]


def offsets(size):
    held = [0]
    for mask in masks(size):
        held = held + [at ^ mask for at in held]
    return held


def gather_rows(rows, axis):
    for mask in masks(lax.axis_size(axis)):
        rows = jnp.concatenate([rows, swap(rows, axis, mask)], axis=0)
    return rows


def scatter_rows(make, count, axis):
    todo = list(reversed(masks(lax.axis_size(axis))))
    half = count // 2
    there = swap(low(make(half, count)), axis, todo[0])
    rows = make(0, half) + wide(there)
    for mask in todo[1:]:
        half = rows.shape[0] // 2
        rows = rows[:half] + wide(swap(low(rows[half:]), axis, mask))
    return rows


def scatter_both(make, count):
    rows = scatter_rows(make, count, "ctx")
    size = lax.axis_size("tp")
    me = lax.axis_index("tp")
    for mask in masks(size):
        half = rows.shape[0] // 2
        upper = (me & mask) != 0
        mine = jnp.where(upper, rows[half:], rows[:half])
        other = jnp.where(upper, rows[:half], rows[half:])
        rows = mine + wide(swap(low(other), "tp", mask))
    return rows


def join_tp(rows):
    size = lax.axis_size("tp")
    me = lax.axis_index("tp")
    for mask in reversed(masks(size)):
        upper = (me & mask) != 0
        other = swap(rows, "tp", mask)
        rows = jnp.where(upper, jnp.concatenate([other, rows], 0), jnp.concatenate([rows, other], 0))
    return rows


def own_part(rows):
    size = lax.axis_size("tp")
    count = rows.shape[0] // size
    return lax.dynamic_slice_in_dim(rows, lax.axis_index("tp") * count, count, 0)


MESH = pl.DeviceIdType.MESH
TILE = 512


def fits_kernels():
    return lax.axis_size("ctx") == 4 and lax.axis_size("tp") == 2


class Place:
    def __init__(self):
        me = lax.axis_index("ctx")
        x, core = me // 2, me % 2
        self.tp = lax.axis_index("tp")
        self.x = {"ctx": (1 - x) * 2 + core}
        self.core = {"ctx": x * 2 + 1 - core}
        self.cross = {"ctx": (1 - x) * 2 + 1 - core}
        self.y = {"tp": 1 - self.tp}

    def others(self, axis):
        size, me = lax.axis_size(axis), lax.axis_index(axis)
        return [{axis: (me + n) % size} for n in range(1, size)]


def meet(devices):
    barrier = pltpu.get_barrier_semaphore()
    for device in devices:
        pl.semaphore_signal(barrier, inc=1, device_id=device, device_id_type=MESH)
    pl.semaphore_wait(barrier, len(devices))


class Links:
    def __init__(self, send, recv):
        self.send, self.recv, self.count, self.sent = send, recv, 0, []

    def copy(self, src, dst, device, at=None):
        n = self.count
        self.count += 1
        made = pltpu.make_async_remote_copy(src, dst, self.send.at[n], self.recv.at[n], device_id=device, device_id_type=MESH)
        self.sent.append(made)
        return made

    def drain(self):
        for made in self.sent:
            made.wait_send()


def start_kernel(hidden, grads, segs, gains, attn_in, cot, segs_out, gains_out, hbuf, nbuf, gbuf, gain_row, send, recv, local_sem):
    place, links = Place(), Links(send, recv)
    rows = hidden.shape[0]
    half, quarter = rows // 2, rows // 4
    z = lax.axis_index("fsdp")
    near = [place.x, place.core, place.cross, place.y]
    far = place.others("fsdp")
    meet(near + far)

    def span(block, part, chunk=None):
        if chunk is None:
            return aligned(block * rows + part * half, half)
        return aligned(block * rows + part * half + chunk * quarter, quarter)

    mine, other = place.tp, 1 - place.tp
    tiny = [links.copy(gains, gains_out.at[z], device) for device in far]
    tiny_segs = [links.copy(segs, segs_out.at[n + 1], device) for n, device in enumerate(near[:3])]
    for made in tiny + tiny_segs:
        made.start()
    over_x = {}
    for name, src, dst in (("h", hidden, hbuf), ("g", grads, gbuf)):
        for q in range(2):
            over_x[name, q] = links.copy(src.at[span(0, mine, q)], dst.at[span(1, mine, q)], place.x)
    over_core = {name: links.copy(src, dst.at[aligned(2 * rows, rows)], place.core) for name, src, dst in (("h", hidden, hbuf), ("g", grads, gbuf))}
    for key in (("h", 0), ("h", 1)):
        over_x[key].start()
    over_core["h"].start()
    for key in (("g", 0), ("g", 1)):
        over_x[key].start()
    over_core["g"].start()
    kept = []

    def keep(src, dst):
        made = pltpu.make_async_copy(src, dst, local_sem.at[len(kept)])
        made.start()
        kept.append(made)

    keep(grads, cot.at[aligned(0, rows)])
    gains_out[z] = gains[...]
    segs_out[0] = segs[...]
    for made in tiny:
        made.wait_recv()
    lanes = 128
    groups = gains.shape[0] // 2
    for device in range(gains_out.shape[0]):
        for row in range(groups):
            gain_row[:, pl.ds((device * groups + row) * lanes, lanes)] = gains_out[device, row : row + 1, :]

    def normalize(src, at, block, count):
        def some(n, _):
            there = aligned(at + n * 64, 64)
            values = wide(src[there, :])
            scale = lax.rsqrt(jnp.mean(values * values, axis=1, keepdims=True) + EPS)
            nbuf[aligned(block + n * 64, 64), :] = low(values * scale * gain_row[...])
            return 0

        lax.fori_loop(0, count // 64, some, 0)
        keep(nbuf.at[pl.ds(block, count)], attn_in.at[pl.ds(block, count)])

    normalize(hidden, 0, 0, rows)
    over_y, across, last = {}, {}, {}

    def pass_on(name, buf):
        for q in range(2):
            over_x[name, q].wait_recv()
            over_y[name, q] = links.copy(buf.at[span(1, mine, q)], buf.at[span(1, mine, q)], place.y)
            across[name, q] = links.copy(buf.at[span(1, mine, q)], buf.at[span(3, mine, q)], place.core)
            over_y[name, q].start()
            across[name, q].start()

    def finish(name, buf):
        for q in range(2):
            over_y[name, q].wait_recv()
            last[name, q] = links.copy(buf.at[span(1, other, q)], buf.at[span(3, other, q)], place.core)
            last[name, q].start()

    pass_on("h", hbuf)
    over_core["h"].wait_recv()
    normalize(hbuf, 2 * rows, 2 * rows, rows)
    finish("h", hbuf)
    normalize(hbuf, rows, rows, rows)
    pass_on("g", gbuf)
    for q in range(2):
        across["h", q].wait_recv()
        last["h", q].wait_recv()
    normalize(hbuf, 3 * rows, 3 * rows, rows)
    over_core["g"].wait_recv()
    keep(gbuf.at[aligned(2 * rows, rows)], cot.at[aligned(2 * rows, rows)])
    finish("g", gbuf)
    keep(gbuf.at[aligned(rows, rows)], cot.at[aligned(rows, rows)])
    for q in range(2):
        across["g", q].wait_recv()
        last["g", q].wait_recv()
    keep(gbuf.at[aligned(3 * rows, rows)], cot.at[aligned(3 * rows, rows)])
    for made in tiny_segs:
        made.wait_recv()
    links.drain()
    for made in kept:
        made.wait()


def start_exchange(hidden, grads, segments, attn_gain, mlp_gain):
    rows, width = hidden.shape
    fsdp = lax.axis_size("fsdp")
    segs = jnp.concatenate([segments.reshape(-1, 128), jnp.zeros((8 - rows // 128, 128), jnp.int32)], axis=0)
    gains = wide(jnp.concatenate([attn_gain, mlp_gain])).reshape(-1, 128)
    vmem = pl.BlockSpec(memory_space=pltpu.VMEM)
    hbm = pl.BlockSpec(memory_space=pl.ANY)
    tokens = 4 * rows
    attn_in, cot, segs, gains = pl.pallas_call(
        start_kernel,
        in_specs=[vmem] * 4,
        out_specs=[hbm, hbm, vmem, vmem],
        out_shape=[
            jax.ShapeDtypeStruct((tokens, width), jnp.bfloat16),
            jax.ShapeDtypeStruct((tokens, width), jnp.bfloat16),
            jax.ShapeDtypeStruct((4, 8, 128), jnp.int32),
            jax.ShapeDtypeStruct((fsdp,) + gains.shape, jnp.float32),
        ],
        scratch_shapes=[
            pltpu.VMEM((tokens, width), jnp.bfloat16),
            pltpu.VMEM((tokens, width), jnp.bfloat16),
            pltpu.VMEM((tokens, width), jnp.bfloat16),
            pltpu.VMEM((1, width), jnp.float32),
            pltpu.SemaphoreType.DMA((fsdp + 32,)),
            pltpu.SemaphoreType.DMA((fsdp + 32,)),
            pltpu.SemaphoreType.DMA((8,)),
        ],
        compiler_params=pltpu.CompilerParams(collective_id=0, has_side_effects=True, vmem_limit_bytes=VMEM_LIMIT),
        cost_estimate=pl.CostEstimate(flops=0, bytes_accessed=200_000_000, transcendentals=0),
    )(hidden, grads, segs, gains)
    segs = segs[:, : rows // 128].reshape(tokens)
    gains = jnp.transpose(gains.reshape(fsdp, 2, -1), (1, 0, 2)).reshape(2, width)
    return attn_in, cot, segs, gains


def scatter_scratch(rows, width):
    part, half = rows // 8, width // 2
    return [
        pltpu.VMEM((4, part, width), jnp.bfloat16),
        pltpu.VMEM((4, part, width), jnp.bfloat16),
        pltpu.VMEM((6, part, half), jnp.bfloat16),
        pltpu.VMEM((6, part, half), jnp.bfloat16),
        pltpu.VMEM((2, part, half), jnp.float32),
        pltpu.VMEM((part, width), jnp.float32),
        pltpu.SemaphoreType.DMA((14,)),
        pltpu.SemaphoreType.DMA((14,)),
    ]


class Scatter:
    def __init__(self, place, make, count, refs, first=("x", "y")):
        self.place, self.make = place, make
        self.hi, self.core_in, self.out, self.come, self.wait, self.total, send, recv = refs
        self.part = count // 8
        self.half = self.total.shape[1] // 2
        self.links = Links(send, recv)
        self.core = {}
        for side in range(2):
            cols = pl.ds(side * self.half, self.half)
            for n in range(4):
                self.core[n, side] = self.links.copy(self.hi.at[n, :, cols], self.core_in.at[n, :, cols], place.core)
        self.send, self.away, self.stays = [], {}, {}
        for side, link in enumerate(first):
            to, then = (place.x, place.y) if link == "x" else (place.y, place.x)
            for n, device in enumerate((to, to, then)):
                at = 3 * side + n
                self.send.append(self.links.copy(self.out.at[at], self.come.at[at], device))
            second, stay = (1, 2) if link == "x" else (2, 1)
            self.away[0, side], self.away[second, side] = 3 * side, 3 * side + 1
            self.stays[side] = stay

    def rows(self, n):
        tp = self.place.tp
        part = (1 - tp) + (n % 2) * (2 * tp - 1)
        return ((1 - n // 2) * 2 + part) * self.part

    def columns(self, side, each):
        tiles = self.half // TILE

        def one(n, _):
            each(aligned(side * self.half + n * TILE, TILE), aligned(n * TILE, TILE))
            return 0

        lax.fori_loop(0, tiles, one, 0)

    def to_core(self, n, side):
        rows = aligned(4 * self.part + self.rows(n), self.part)

        def each(cols, _):
            self.hi[n, :, cols] = low(self.make(rows, cols))

        self.columns(side, each)
        self.core[n, side].start()

    def to_links(self, n, side):
        rows = aligned(self.rows(n), self.part)
        self.core[n, side].wait_recv()

        def each(cols, at):
            value = self.make(rows, cols) + wide(self.core_in[n, :, cols])
            if (n, side) in self.away:
                self.out[self.away[n, side], :, at] = low(value)
            elif n == 3:
                self.total[:, cols] = value
            else:
                self.wait[side, :, at] = value

        self.columns(side, each)
        if (n, side) in self.away:
            self.send[self.away[n, side]].start()

    def units(self):
        return (
            [(0, side) for side in range(2)]
            + [(n, side) for n in (1, 2) for side in range(2) if (n, side) in self.away]
            + [(self.stays[side], side) for side in range(2)]
            + [(3, side) for side in range(2)]
        )

    def start(self, waits=()):
        units = self.units()
        ahead = 2
        waits = list(waits) + [()] * 3
        for at, unit in enumerate(units[:ahead]):
            for made in waits[at]:
                made.wait()
            self.to_core(*unit)
        for made in waits[2]:
            made.wait()
        for at, unit in enumerate(units):
            self.to_links(*unit)
            if at + ahead < len(units):
                self.to_core(*units[at + ahead])

    def turn(self):
        for side in range(2):
            came, goes = 3 * side, 3 * side + 2
            self.send[came].wait_recv()

            def each(_, at):
                self.out[goes, :, at] = low(self.wait[side, :, at] + wide(self.come[came, :, at]))

            self.columns(side, each)
            self.send[goes].start()

    def finish(self):
        for side in range(2):
            for n in (1, 2):
                self.send[3 * side + n].wait_recv()
            cols = pl.ds(side * self.half, self.half)
            self.total[:, cols] = self.total[:, cols] + wide(self.come[3 * side + 1]) + wide(self.come[3 * side + 2])
        self.links.drain()


def gather_plane(place, links, mine, full, part):
    half = mine.shape[1] // 2
    left, right = pl.ds(0, half), pl.ds(half, half)
    own, other = place.tp, 1 - place.tp

    def rows(block, tp):
        return aligned((block * 2 + tp) * part, part)

    y_left = links.copy(mine.at[:, left], full.at[rows(0, own), left], place.y)
    x_right = links.copy(mine.at[:, right], full.at[rows(1, own), right], place.x)
    y_right = links.copy(mine.at[:, right], full.at[rows(0, own), right], place.y)
    x_left = links.copy(mine.at[:, left], full.at[rows(1, own), left], place.x)
    core = [links.copy(mine, full.at[rows(2, own)], place.core)]
    for made in (y_left, x_right, y_right, x_left, core[0]):
        made.start()

    def relay(come, block, tp, cols, onward=None):
        come.wait_recv()
        here = full.at[rows(block, tp), cols]
        if onward == "x":
            made = links.copy(here, full.at[rows(1, tp), cols], place.x)
        elif onward == "y":
            made = links.copy(here, full.at[rows(block, tp), cols], place.y)
        if onward:
            made.start()
        over = links.copy(here, full.at[rows(block + 2, tp), cols], place.core)
        over.start()
        core.append(over)
        return made if onward else None

    far_left = relay(y_left, 0, other, left, "x")
    far_right = relay(x_right, 1, own, right, "y")
    relay(y_right, 0, other, right)
    relay(x_left, 1, own, left)
    relay(far_left, 1, other, left)
    relay(far_right, 1, other, right)
    for made in core:
        made.wait_recv()


def load(sems, pairs):
    made = [pltpu.make_async_copy(src, dst, sems.at[n]) for n, (src, dst) in enumerate(pairs)]
    for copy in made:
        copy.start()
    return made


def forward_mid_kernel(mixed, weight, hidden, gain, full, resid_out, mine, *refs):
    place = Place()
    scatter_refs, (send, recv, local_sem) = refs[:-3], refs[-3:]
    count = mixed.shape[0]
    part = count // 8
    meet([place.x, place.core, place.y])
    scatter = Scatter(place, lambda rows, cols: contract_cols(mixed[rows, :], weight[cols, weight.shape[1] - mixed.shape[1] :]), count, scatter_refs)
    scatter.start()
    scatter.turn()
    scatter.finish()
    step = 64

    def some(n, _):
        rows = aligned(n * step, step)
        values = wide(hidden[aligned(place.tp * part + n * step, step), :]) + scatter.total[rows, :]
        resid_out[rows, :] = values
        scale = lax.rsqrt(jnp.mean(values * values, axis=1, keepdims=True) + EPS)
        mine[rows, :] = low(values * scale * gain[...])
        return 0

    lax.fori_loop(0, part // step, some, 0)
    stay = pltpu.make_async_copy(mine, full.at[aligned(place.tp * part, part)], local_sem)
    stay.start()
    links = Links(send, recv)
    gather_plane(place, links, mine, full, part)
    links.drain()
    stay.wait()


def mid_scratch(count, width):
    return [pltpu.VMEM((count // 8, width), jnp.bfloat16)] + scatter_scratch(count, width) + [
        pltpu.SemaphoreType.DMA((16,)),
        pltpu.SemaphoreType.DMA((16,)),
        pltpu.SemaphoreType.DMA,
    ]


def forward_mid(mixed, weight, hidden, gain):
    count, width = mixed.shape[0], weight.shape[0]
    vmem = pl.BlockSpec(memory_space=pltpu.VMEM)
    return pl.pallas_call(
        forward_mid_kernel,
        in_specs=[vmem] * 4,
        out_specs=[pl.BlockSpec(memory_space=pl.ANY), vmem],
        out_shape=[jax.ShapeDtypeStruct((count, width), jnp.bfloat16), jax.ShapeDtypeStruct((count // 8, width), jnp.float32)],
        scratch_shapes=mid_scratch(count, width),
        compiler_params=pltpu.CompilerParams(collective_id=1, has_side_effects=True, vmem_limit_bytes=VMEM_LIMIT),
        cost_estimate=pl.CostEstimate(flops=0, bytes_accessed=300_000_000, transcendentals=0),
    )(mixed, weight, hidden, gain[None, :])


def norm_back(values, scale, gain, cot):
    scaled = cot * gain
    lean = jnp.mean(values * scaled, axis=1, keepdims=True)
    return scale * scaled - values * (scale * scale * scale) * lean, cot * (values * scale)


def backward_mid_kernel(
    gate_hbm, up_hbm, weights_hbm, resid_hbm, grads_hbm, gain, full, cot_out, gain_out,
    gate_cot, up_cot, weights, resid, grads, sems, mine, *refs
):
    place = Place()
    scatter_refs, (send, recv, local_sem) = refs[:-3], refs[-3:]
    count, hidden_cols = gate_cot.shape
    part = count // 8
    width = weights.shape[0]
    lower, upper = pl.ds(0, count // 2), pl.ds(count // 2, count // 2)
    left, right = pl.ds(0, width // 2), pl.ds(width // 2, width // 2)
    loads = load(
        sems,
        [
            (weights_hbm.at[left], weights.at[left]),
            (gate_hbm.at[upper], gate_cot.at[upper]),
            (up_hbm.at[upper], up_cot.at[upper]),
            (weights_hbm.at[right], weights.at[right]),
            (gate_hbm.at[lower], gate_cot.at[lower]),
            (up_hbm.at[lower], up_cot.at[lower]),
            (resid_hbm, resid),
            (grads_hbm.at[aligned(place.tp * part, part)], grads),
        ],
    )
    meet([place.x, place.core, place.y])

    def make(rows, cols):
        return contract_cols(gate_cot[rows, :], weights[cols, :hidden_cols]) + contract_cols(up_cot[rows, :], weights[cols, hidden_cols:])

    scatter = Scatter(place, make, count, scatter_refs)
    scatter.start((loads[:3], loads[3:4], loads[4:6]))
    scatter.turn()
    scatter.finish()
    for made in loads[6:]:
        made.wait()
    step = 32

    def some(n, sums):
        rows = aligned(n * step, step)
        values = resid[rows, :]
        scale = lax.rsqrt(jnp.mean(values * values, axis=1, keepdims=True) + EPS)
        back, terms = norm_back(values, scale, gain[...], scatter.total[rows, :])
        cot = wide(grads[rows, :]) + back
        cot_out[rows, :] = cot
        mine[rows, :] = low(cot)
        return sums + jnp.sum(terms, axis=0, keepdims=True)

    gain_out[...] = lax.fori_loop(0, part // step, some, jnp.zeros(gain.shape, jnp.float32))
    stay = pltpu.make_async_copy(mine, full.at[aligned(place.tp * part, part)], local_sem)
    stay.start()
    links = Links(send, recv)
    gather_plane(place, links, mine, full, part)
    links.drain()
    stay.wait()


def backward_mid(gate_cot, up_cot, weights, resid, grads, gain):
    count, width = gate_cot.shape[0], weights.shape[0]
    vmem = pl.BlockSpec(memory_space=pltpu.VMEM)
    hbm = pl.BlockSpec(memory_space=pl.ANY)
    return pl.pallas_call(
        backward_mid_kernel,
        in_specs=[hbm] * 5 + [vmem],
        out_specs=[pl.BlockSpec(memory_space=pl.ANY), vmem, vmem],
        out_shape=[
            jax.ShapeDtypeStruct((count, width), jnp.bfloat16),
            jax.ShapeDtypeStruct((count // 8, width), jnp.float32),
            jax.ShapeDtypeStruct((1, width), jnp.float32),
        ],
        scratch_shapes=[
            pltpu.VMEM(gate_cot.shape, jnp.bfloat16),
            pltpu.VMEM(up_cot.shape, jnp.bfloat16),
            pltpu.VMEM(weights.shape, jnp.bfloat16),
            pltpu.VMEM(resid.shape, jnp.float32),
            pltpu.VMEM(resid.shape, jnp.bfloat16),
            pltpu.SemaphoreType.DMA((8,)),
        ]
        + mid_scratch(count, width),
        compiler_params=pltpu.CompilerParams(collective_id=2, has_side_effects=True, vmem_limit_bytes=VMEM_LIMIT),
        cost_estimate=pl.CostEstimate(flops=0, bytes_accessed=300_000_000, transcendentals=0),
    )(gate_cot, up_cot, weights, resid, grads, gain[None, :])


def input_kernel(cots, weights, cot_hbm, hidden_hbm, gain, gain_two, grad_out, gains_out, resid_cot, hidden, sems, sums, come, *refs):
    place = Place()
    (send, recv), refs = refs[-2:], refs[:-2]
    count = cots.shape[0]
    part = count // 8
    loads = load(sems, [(cot_hbm, resid_cot), (hidden_hbm.at[aligned(place.tp * part, part)], hidden)])
    meet([place.x, place.core, place.y] + place.others("fsdp"))
    scatter = Scatter(place, lambda rows, cols: contract_cols(cots[rows, :], weights[cols, : cots.shape[1]]), count, refs, ("y", "y"))
    links = Links(send, recv)
    scatter.start()
    scatter.turn()
    scatter.finish()
    for made in loads:
        made.wait()
    step = 32

    def some(n, total):
        rows = aligned(n * step, step)
        values = wide(hidden[rows, :])
        scale = lax.rsqrt(jnp.mean(values * values, axis=1, keepdims=True) + EPS)
        back, terms = norm_back(values, scale, gain[...], scatter.total[rows, :])
        grad_out[rows, :] = low(resid_cot[rows, :] + back)
        return total + jnp.sum(terms, axis=0, keepdims=True)

    sums[0, 0:1, :] = lax.fori_loop(0, part // step, some, jnp.zeros(gain.shape, jnp.float32))
    sums[0, 1:2, :] = gain_two[...]
    near = [place.x, place.core, place.y]
    for n, device in enumerate(near):
        made = links.copy(sums.at[n], come.at[n], device)
        made.start()
        made.wait_recv()
        sums[n + 1] = sums[n] + come[n]
    at = len(near)
    far = [links.copy(sums.at[at], come.at[at + n], device) for n, device in enumerate(place.others("fsdp"))]
    for made in far:
        made.start()
    total = sums[at]
    for n, made in enumerate(far):
        made.wait_recv()
        total = total + come[at + n]
    gains_out[...] = total
    links.drain()


def input_exchange(cots, weights, resid_cot, hidden, gain, gain_two):
    count, width = cots.shape[0], weights.shape[0]
    fsdp = lax.axis_size("fsdp")
    vmem = pl.BlockSpec(memory_space=pltpu.VMEM)
    return pl.pallas_call(
        input_kernel,
        in_specs=[vmem] * 2 + [pl.BlockSpec(memory_space=pl.ANY)] * 2 + [vmem] * 2,
        out_specs=[vmem, vmem],
        out_shape=[jax.ShapeDtypeStruct((count // 8, width), jnp.bfloat16), jax.ShapeDtypeStruct((2, width), jnp.float32)],
        scratch_shapes=[
            pltpu.VMEM(resid_cot.shape, jnp.float32),
            pltpu.VMEM(resid_cot.shape, jnp.bfloat16),
            pltpu.SemaphoreType.DMA((2,)),
            pltpu.VMEM((4, 2, width), jnp.float32),
            pltpu.VMEM((2 + fsdp, 2, width), jnp.float32),
        ]
        + scatter_scratch(count, width)
        + [pltpu.SemaphoreType.DMA((4 + fsdp,)), pltpu.SemaphoreType.DMA((4 + fsdp,))],
        compiler_params=pltpu.CompilerParams(collective_id=3, has_side_effects=True, vmem_limit_bytes=VMEM_LIMIT),
        cost_estimate=pl.CostEstimate(flops=0, bytes_accessed=180_000_000, transcendentals=0),
    )(cots, weights, resid_cot, hidden, gain[None, :], gain_two)


def attention_output_kernel(
    rot_hbm, cos_hbm, sin_hbm, seg_col, seg_row, cot_hbm, mixed_hbm, lse, hidden_act, down, resid_hbm, cots, out,
    rot, cos, sin, cot, mixed, resid, sems, delta, dq, *refs
):
    place = Place()
    count = hidden_act.shape[0]
    me = lax.axis_index("ctx")
    blocks = count // BLOCK
    per = count // 4 // BLOCK

    def at(block):
        n = block // per
        return (((me // 2 + n % 2) % 2) * 2 + (me % 2 + n // 2) % 2) * per + block % per

    def follows(i, j):
        return (at(j) < at(i)) & (at(i) - at(j) <= blocks // 2)

    loads = load(
        sems, [(rot_hbm, rot), (cos_hbm, cos), (sin_hbm, sin), (cot_hbm, cot), (mixed_hbm, mixed), (resid_hbm, resid)]
    )
    meet([place.x, place.core, place.y])
    scatter = Scatter(place, lambda rows, cols: product(hidden_act[rows, :], down[:, cols]), count, refs, ("y", "y"))
    scatter.start()
    for made in loads:
        made.wait()
    pairs = rot.shape[1] // (3 * PAIR)
    steps = pairs * blocks

    def step(n, _):
        back = Backward(n // blocks, rot, cos, sin, seg_col, seg_row, cot, mixed, lse, cots, delta, dq, follows)

        @pl.when(n % blocks == 0)
        def _():
            back.prepare()

        back.column(n % blocks)

        @pl.when(n % blocks == blocks - 1)
        def _():
            back.finish()

        @pl.when(n == steps // 4 - 1)
        def _():
            scatter.turn()

        return 0

    lax.fori_loop(0, steps, step, 0)
    scatter.finish()
    out[...] = low(resid[...] + scatter.total[...])


def attention_output(rot, cos, sin, seg_col, seg_row, cot, mixed, lse, hidden_act, down, resid):
    count, width = hidden_act.shape[0], down.shape[1]
    vmem = pl.BlockSpec(memory_space=pltpu.VMEM)
    hbm = pl.BlockSpec(memory_space=pl.ANY)
    return pl.pallas_call(
        attention_output_kernel,
        in_specs=[hbm] * 3 + [vmem] * 2 + [hbm] * 2 + [vmem] * 3 + [hbm],
        out_specs=[vmem, vmem],
        out_shape=[
            jax.ShapeDtypeStruct(rot.shape, jnp.bfloat16),
            jax.ShapeDtypeStruct((count // 8, width), jnp.bfloat16),
        ],
        scratch_shapes=[pltpu.VMEM(array.shape, array.dtype) for array in (rot, cos, sin, cot, mixed, resid)]
        + [
            pltpu.SemaphoreType.DMA((6,)),
            pltpu.VMEM((2, count), jnp.float32),
            pltpu.VMEM((count, PAIR), jnp.float32),
        ]
        + scatter_scratch(count, width),
        compiler_params=pltpu.CompilerParams(collective_id=4, has_side_effects=True, vmem_limit_bytes=VMEM_LIMIT),
        cost_estimate=pl.CostEstimate(flops=0, bytes_accessed=220_000_000, transcendentals=0),
    )(rot, cos, sin, seg_col, seg_row, cot, mixed, lse, hidden_act, down, resid)


def take_attention_kernel(at, query, key, value, out, taken):
    pairs = query.shape[1] // PAIR
    for p in range(pairs):
        for n, part in enumerate((query, key, value)):
            taken[:, (3 * p + n) * PAIR : (3 * p + n + 1) * PAIR] = part[:, p * PAIR : (p + 1) * PAIR]
    taken[:, 3 * pairs * PAIR :] = out[...].T


def take_attention(me, query, key, value, out, count):
    depth = query.shape[0]
    block = pl.BlockSpec((depth, count), lambda n, at: (0, at[0]))
    return pl.pallas_call(
        take_attention_kernel,
        grid_spec=pltpu.PrefetchScalarGridSpec(
            num_scalar_prefetch=1,
            grid=(1,),
            in_specs=[block] * 3 + [pl.BlockSpec((count, depth), lambda n, at: (at[0], 0))],
            out_specs=pl.BlockSpec((depth, 4 * count), lambda n, at: (0, 0)),
        ),
        out_shape=jax.ShapeDtypeStruct((depth, 4 * count), query.dtype),
        compiler_params=pltpu.CompilerParams(vmem_limit_bytes=VMEM_LIMIT),
    )(me, query, key, value, out)


def take_hidden_kernel(at, gate, up, down, both, rows):
    count = gate.shape[1]
    both[:, :count] = gate[...]
    both[:, count:] = up[...]
    rows[...] = down[...]


def take_hidden(me, gate, up, down, count):
    depth = gate.shape[0]
    block = pl.BlockSpec((depth, count), lambda n, at: (0, at[0]))
    return pl.pallas_call(
        take_hidden_kernel,
        grid_spec=pltpu.PrefetchScalarGridSpec(
            num_scalar_prefetch=1,
            grid=(1,),
            in_specs=[block] * 2 + [pl.BlockSpec((count, depth), lambda n, at: (at[0], 0))],
            out_specs=[pl.BlockSpec((depth, 2 * count), lambda n, at: (0, 0)), pl.BlockSpec((count, depth), lambda n, at: (0, 0))],
        ),
        out_shape=[jax.ShapeDtypeStruct((depth, 2 * count), gate.dtype), jax.ShapeDtypeStruct((count, depth), down.dtype)],
        compiler_params=pltpu.CompilerParams(vmem_limit_bytes=VMEM_LIMIT),
    )(me, gate, up, down)


def first_swaps(block):
    pieces = [block]
    for mask in masks(lax.axis_size("ctx"))[:-1]:
        pieces = pieces + [swap(piece, "ctx", mask) for piece in pieces]
    return pieces


def last_swap(pieces):
    return pieces + [swap(piece, "ctx", 1) for piece in pieces]


def order_of_pieces():
    return lax.axis_index("ctx") ^ jnp.array(offsets(lax.axis_size("ctx")), jnp.int32)


def place_kernel(at, *refs):
    out = refs[-1]
    for n, piece in enumerate(refs[:-1]):

        @pl.when(pl.program_id(0) == n)
        def _():
            out[...] = wide(piece[...])


def place_pieces(pieces, axis):
    block = pieces[0].shape
    shape = list(block)
    shape[axis] *= len(pieces)
    return pl.pallas_call(
        place_kernel,
        grid_spec=pltpu.PrefetchScalarGridSpec(
            num_scalar_prefetch=1,
            grid=(len(pieces),),
            in_specs=[pl.BlockSpec(block, lambda n, at: (0, 0))] * len(pieces),
            out_specs=pl.BlockSpec(block, lambda n, at: (at[n], 0) if axis == 0 else (0, at[n])),
        ),
        out_shape=jax.ShapeDtypeStruct(shape, jnp.float32),
        compiler_params=pltpu.CompilerParams(vmem_limit_bytes=VMEM_LIMIT),
        cost_estimate=pl.CostEstimate(flops=0, bytes_accessed=6 * math.prod(shape), transcendentals=0),
    )(order_of_pieces(), *pieces)


def place_gate_up_kernel(at, *refs):
    pieces, (gate, up) = refs[:-2], refs[-2:]
    count = gate.shape[1]
    for n, piece in enumerate(pieces):

        @pl.when(pl.program_id(0) == n)
        def _():
            gate[...] = wide(piece[:, :count])
            up[...] = wide(piece[:, count:])


def place_gate_up(pieces):
    rows, cols = pieces[0].shape
    count, whole = cols // 2, cols // 2 * len(pieces)
    side = pl.BlockSpec((rows, count), lambda n, at: (0, at[n]))
    return pl.pallas_call(
        place_gate_up_kernel,
        grid_spec=pltpu.PrefetchScalarGridSpec(
            num_scalar_prefetch=1,
            grid=(len(pieces),),
            in_specs=[pl.BlockSpec((rows, cols), lambda n, at: (0, 0))] * len(pieces),
            out_specs=[side] * 2,
        ),
        out_shape=[jax.ShapeDtypeStruct((rows, whole), jnp.float32)] * 2,
        compiler_params=pltpu.CompilerParams(vmem_limit_bytes=VMEM_LIMIT),
        cost_estimate=pl.CostEstimate(flops=0, bytes_accessed=12 * rows * whole, transcendentals=0),
    )(order_of_pieces(), *pieces)


def place_attention_kernel(at, *refs):
    pieces, outs = refs[:-4], refs[-4:]
    count = outs[0].shape[1]
    pairs = count // PAIR
    for n, piece in enumerate(pieces):

        @pl.when(pl.program_id(0) == n)
        def _():
            for p in range(pairs):
                for m in range(3):
                    outs[m][:, p * PAIR : (p + 1) * PAIR] = wide(piece[:, (3 * p + m) * PAIR : (3 * p + m + 1) * PAIR])
            outs[3][...] = wide(piece[:, 3 * count :]).T


def place_attention(pieces):
    depth, count = pieces[0].shape[0], pieces[0].shape[1] // 4
    whole = len(pieces) * count
    side = pl.BlockSpec((depth, count), lambda n, at: (0, at[n]))
    return pl.pallas_call(
        place_attention_kernel,
        grid_spec=pltpu.PrefetchScalarGridSpec(
            num_scalar_prefetch=1,
            grid=(len(pieces),),
            in_specs=[pl.BlockSpec(pieces[0].shape, lambda n, at: (0, 0))] * len(pieces),
            out_specs=[side] * 3 + [pl.BlockSpec((count, depth), lambda n, at: (at[n], 0))],
        ),
        out_shape=[jax.ShapeDtypeStruct((depth, whole), jnp.float32)] * 3 + [jax.ShapeDtypeStruct((whole, depth), jnp.float32)],
        compiler_params=pltpu.CompilerParams(vmem_limit_bytes=VMEM_LIMIT),
        cost_estimate=pl.CostEstimate(flops=0, bytes_accessed=24 * depth * whole, transcendentals=0),
    )(order_of_pieces(), *pieces)


def local(
    hidden_in,
    out_grad,
    segment_ids,
    attn_gain,
    w_query,
    w_key,
    w_value,
    w_out,
    mlp_gain,
    w_gate,
    w_up,
    w_down,
):
    group = lax.axis_size("ctx")
    me = lax.axis_index("ctx")
    local_rows = hidden_in.shape[1]
    tokens = local_rows * group
    head_cols = w_query.shape[1] // group
    ff_cols = w_gate.shape[1] // group

    def gather(weight, axis):
        return lax.all_gather(weight, "fsdp", axis=axis, tiled=True)

    def settle(part, axis):
        return lax.psum_scatter(part, "fsdp", scatter_dimension=axis, tiled=True)

    at = me[None]
    w_attn = gather(take_attention(at, w_query, w_key, w_value, w_out, head_cols), 0)
    qkv_cols = 3 * head_cols
    w_qkv, w_out_t = w_attn[:, :qkv_cols], w_attn[:, qkv_cols:]
    own_gate_up, own_down = take_hidden(at, w_gate, w_up, w_down, ff_cols)
    full_gate_up = gather(own_gate_up, 0)
    full_down = gather(own_down, 1)

    kernels = fits_kernels()
    if kernels:
        attn_in, branch_cot, segments, gains = start_exchange(hidden_in[0], out_grad[0], segment_ids[0], attn_gain, mlp_gain)
        gain_one, gain_two = gains[0], gains[1]
    else:
        gains = wide(gather(jnp.stack([attn_gain, mlp_gain]), 1))
        gain_one, gain_two = gains[0], gains[1]
        rows_in = wide(hidden_in[0])
        r1 = lax.rsqrt(jnp.mean(rows_in * rows_in, axis=-1, keepdims=True) + EPS)
        attn_in = gather_rows(low(rows_in * r1 * gain_one), "ctx")
        segments = gather_rows(segment_ids[0], "ctx")
        branch_cot = gather_rows(out_grad[0], "ctx")

    firsts = jnp.stack([(me ^ at) * local_rows for at in offsets(group)])
    positions = (firsts[:, None] + jnp.arange(local_rows, dtype=jnp.int32)[None, :]).reshape(tokens)
    exponents = jnp.arange(0, HEAD_DIM, 2).astype(jnp.float32) / HEAD_DIM
    inverse = jnp.float32(ROPE_BASE) ** (-exponents)
    angles = positions.astype(jnp.float32)[:, None] * inverse[None, :]
    cos = jnp.tile(jnp.cos(angles), (1, 4))
    sin = jnp.tile(jnp.sin(angles), (1, 4))
    info = jnp.stack([positions[::BLOCK], segments[::BLOCK], segments[BLOCK - 1 :: BLOCK]])
    seg_col, seg_row = segments[:, None], segments[None, :]

    qkv = product(attn_in, w_qkv)
    rot, mixed, mixed_wide, lse = attention_forward(info, qkv, cos, sin, seg_col, seg_row)

    own_in = wide(own_part(hidden_in[0]))
    if kernels:
        mlp_in, resid = forward_mid(mixed, w_attn, hidden_in[0], gain_two)
    else:
        part = scatter_both(lambda lo, hi: contract_cols(mixed[lo:hi], w_out_t), tokens)
        resid = own_in + part
        r2 = lax.rsqrt(jnp.mean(resid * resid, axis=-1, keepdims=True) + EPS)
        mlp_in = gather_rows(join_tp(low(resid * r2 * gain_two)), "ctx")
    acts = product(mlp_in, full_gate_up)
    gate_act, up_act = acts[:, :ff_cols], acts[:, ff_cols:]
    sigmoid = jax.nn.sigmoid(gate_act)
    hidden = low(gate_act * sigmoid * up_act)
    gate_slope = low(up_act * sigmoid * (1.0 + gate_act * (1.0 - sigmoid)))
    up_slope = low(gate_act * sigmoid)
    hidden, gate_slope, up_slope = lax.optimization_barrier((hidden, gate_slope, up_slope))
    down_part = low(contract_rows(hidden, branch_cot))
    down_part, full_down, branch_cot = lax.optimization_barrier((down_part, full_down, branch_cot))
    down_own = settle(down_part, 1)

    hidden_cot = contract_cols(branch_cot, full_down)
    gate_cot = low(hidden_cot * gate_slope)
    up_cot = low(hidden_cot * up_slope)
    gate_up_part = jnp.concatenate([low(contract_rows(mlp_in, gate_cot)), low(contract_rows(mlp_in, up_cot))], axis=1)
    gate_up_own = settle(gate_up_part, 0)
    if kernels:
        gate_cot, up_cot, gate_up_part = lax.optimization_barrier((gate_cot, up_cot, gate_up_part))
        attn_cot, resid_cot, gain_two_part = backward_mid(gate_cot, up_cot, full_gate_up, resid, out_grad[0], gain_two)
    else:
        mlp_in_cot = scatter_both(
            lambda lo, hi: contract_cols(gate_cot[lo:hi], full_gate_up[:, :ff_cols])
            + contract_cols(up_cot[lo:hi], full_gate_up[:, ff_cols:]),
            tokens,
        )
        back, terms = norm_back(resid, r2, gain_two, mlp_in_cot)
        gain_two_part = jnp.sum(terms, axis=0, keepdims=True)
        resid_cot = wide(own_part(out_grad[0])) + back
        attn_cot = gather_rows(join_tp(low(resid_cot)), "ctx")
    mixed_cot = low(product(attn_cot, w_out_t))
    out_part = low(contract_rows(attn_cot, mixed))
    mixed_cot, out_part, down_own = lax.optimization_barrier((mixed_cot, out_part, down_own))
    down_pieces = first_swaps(down_own)
    if kernels:
        cots, output = attention_output(rot, cos, sin, seg_col, seg_row, mixed_cot, mixed_wide, lse, hidden, full_down, resid)
        output = join_tp(output)
    else:
        cots = attention_backward(info, rot, cos, sin, seg_col, seg_row, mixed_cot, mixed_wide, lse)
    cots, *down_pieces = lax.optimization_barrier((cots, *down_pieces))
    qkv_part = low(contract_rows(attn_in, cots))
    attn_part = jnp.concatenate([qkv_part, out_part], axis=1)
    attn_own = settle(attn_part, 0)
    if kernels:
        cots, attn_part, gate_up_own = lax.optimization_barrier((cots, attn_part, gate_up_own))
        gate_up_pieces = first_swaps(gate_up_own)
        input_grad, gain_sums = input_exchange(cots, w_attn, resid_cot, hidden_in[0], gain_one, gain_two_part)
        input_grad, *gate_up_pieces = lax.optimization_barrier((input_grad, *gate_up_pieces))
        input_grad = join_tp(input_grad)
    else:
        gate_up_pieces = first_swaps(gate_up_own)
        out_sum = scatter_both(lambda lo, hi: product(hidden[lo:hi], full_down), tokens)
        output = join_tp(low(resid + out_sum))
        attn_in_cot = scatter_both(lambda lo, hi: contract_cols(cots[lo:hi], w_qkv), tokens)
        back, terms = norm_back(own_in, own_part(r1), gain_one, attn_in_cot)
        input_grad = join_tp(low(resid_cot + back))
        gain_sums = lax.psum(jnp.concatenate([jnp.sum(terms, axis=0, keepdims=True), gain_two_part]), ("fsdp", "ctx", "tp"))
    attn_pieces = first_swaps(attn_own)
    down_grad = place_pieces(last_swap(down_pieces), 0)
    gate_grad, up_grad = place_gate_up(last_swap(gate_up_pieces))
    down_grad, gate_grad, up_grad, output, *attn_pieces = lax.optimization_barrier(
        (down_grad, gate_grad, up_grad, output, *attn_pieces)
    )
    query_grad, key_grad, value_grad, out_proj_grad = place_attention(last_swap(attn_pieces))

    gain_sums = lax.dynamic_slice_in_dim(gain_sums, lax.axis_index("fsdp") * attn_gain.shape[0], attn_gain.shape[0], 1)
    return (
        output[None],
        input_grad[None],
        gain_sums[0],
        query_grad,
        key_grad,
        value_grad,
        out_proj_grad,
        gain_sums[1],
        gate_grad,
        up_grad,
        down_grad,
    )


def solution(mesh):
    weight, gain = P("fsdp", "tp"), P("fsdp")
    rows = P("fsdp", "ctx", None)
    in_specs = (rows, rows, P("fsdp", "ctx"), gain, weight, weight, weight, P("tp", "fsdp"), gain, weight, weight, P("tp", "fsdp"))
    out_specs = (rows, rows, gain, weight, weight, weight, P("tp", "fsdp"), gain, weight, weight, P("tp", "fsdp"))
    return jax.shard_map(local, mesh=mesh, in_specs=in_specs, out_specs=out_specs, check_vma=False)
```

profile of v0, /device:TPU:0, one launch (start us, length us, event | category | flops | bytes accessed | tf_op | source)
XLA Modules:
  0.0 697.8 jit_solution(12976758989292636768)
XLA Ops:
  7.2 2.4 shard_map.231
  9.7 0.0 all-gather.6.cloned.1.call-start
  9.7 3.7 shard_map.234
  13.5 0.7 all-gather.8.cloned.1.call-update
  14.2 0.6 concatenate.47.segs
  14.8 0.6 maximum_convert_fusion.gains
  15.4 70.5 %shard_map.230 = (bf16[2048,2048]{1,0:T(8,128)(2,1)}, bf16[2048,2048]{1,0:T(8,128)(2,1)}, s32[4,8,128]{2,1,0:T(8,128)}, f32[4,8,128]{2,1,0:T(8,128)}) custom-call(bf16[512,2048]{1,0:T(8,128)(2,1)} %bitcast.51, bf16[512,2048]{1,0:T(8,128)(2,1)} %bitcast.54, s32[8,128]{1,0:T(8,128)} %concatenate.47.segs, f32[8,128]{1,0:T(8,128)} %maximum_convert_fusion.gains), custom_call_target="tpu_custom_call" | custom-call | bytes 200000000 | tf_op jit(solution)/shard_map/pallas_call | solution.py:507
  85.9 0.7 slice.43
  86.7 0.1 slice.44
  86.7 0.1 slice.45
  86.8 0.1 pad_add_fusion.1
  86.9 0.1 add_bitcast_fusion
  87.0 0.1 slice.42
  87.1 1.0 multiply_sine_fusion
  88.1 0.1 tile.8
  88.2 1.3 copy.30.cos_ref.cos_hbm
  89.5 0.1 tile.20
  89.6 1.3 copy.31.sin_ref.sin_hbm
  90.9 1.3 copy.32.seg_col
  92.3 0.6 slice_bitcast_fusion
  92.9 0.6 copy.44
  93.5 0.6 pad_add_fusion.info
  94.1 11.7 %fusion.1.qkv_ref = f32[2048,768]{1,0:T(8,128)} fusion(bf16[2048,2048]{1,0:T(8,128)(2,1)} %get-tuple-element.62, bf16[2048,1024]{1,0:T(8,128)(2,1)} %all-gather.4.cloned.1.call-done.weight.weights), kind=kOutput, calls=%fused_computation.12 | convolution fusion | flops 6442450944 | bytes 17825792 | tf_op jit(solution)/shard_map/dot_general | solution.py:29
  105.8 28.7 %shard_map.232 = (bf16[2048,768]{1,0:T(8,128)(2,1)}, bf16[2048,256]{1,0:T(8,128)(2,1)}, f32[2048,256]{1,0:T(8,128)}, f32[2,2,2048]{2,1,0:T(2,128)}) custom-call(s32[3,4]{1,0:T(4,128)} %pad_add_fusion.info, f32[2048,768]{1,0:T(8,128)} %fusion.1.qkv_ref, f32[2048,128]{1,0:T(8,128)} %copy.30.cos_ref.cos_hbm, f32[2048,128]{1,0:T(8,128)} %copy.31.sin_ref.sin_hbm, ...), custom_call_target="tpu_custom_call" | custom-call | flops 3221225472 | bytes 15728640 | tf_op jit(solution)/shard_map/pallas_call | solution.py:224
  134.5 84.8 %shard_map.233 = (bf16[2048,2048]{1,0:T(8,128)(2,1)}, f32[256,2048]{1,0:T(8,128)}) custom-call(bf16[2048,256]{1,0:T(8,128)(2,1)} %get-tuple-element.64.mixed, bf16[2048,1024]{1,0:T(8,128)(2,1)} %all-gather.4.cloned.1.call-done.weight.weights, bf16[512,2048]{1,0:T(8,128)(2,1)} %bitcast.52, f32[1,2048]{1,0:T(1,128)} %bitcast.65), custom_call_target="tpu_custom_call" | custom-call | bytes 300000000 | tf_op jit(solution)/shard_map/pallas_call | solution.py:740
  219.3 24.8 %all-gather.6.cloned.1.call-done.weights_hbm = bf16[2048,2048]{1,0:T(8,128)(2,1)} async-done(((bf16[512,2048]{1,0:T(8,128)(2,1)}), bf16[2048,2048]{1,0:T(8,128)(2,1)}) %all-gather.6.cloned.1.call-update) | async-done | bytes 8388624 | tf_op jit(solution)/shard_map/all_gather | solution.py:1155
  244.1 21.6 %fusion.6 = f32[2048,2048]{1,0:T(8,128)S(1)} fusion(bf16[2048,2048]{1,0:T(8,128)(2,1)} %get-tuple-element.66, bf16[2048,2048]{1,0:T(8,128)(2,1)} %all-gather.6.cloned.1.call-done.weights_hbm), kind=kOutput, calls=%fused_computation.33 | convolution fusion | flops 17179869184 | bytes 33554432 | tf_op jit(solution)/shard_map/dot_general | solution.py:29
  265.7 5.9 fusion.4
  271.6 2.0 copy-done
  273.6 13.0 %convolution_convert_fusion = bf16[1024,2048]{1,0:T(8,128)(2,1)} fusion(bf16[2048,1024]{1,0:T(8,128)(2,1)S(1)} %get-tuple-element.68.hidden_act, bf16[2048,2048]{1,0:T(8,128)(2,1)} %get-tuple-element.71), kind=kOutput, calls=%fused_computation.8 | convolution fusion | flops 8592031744 | bytes 16777216 | tf_op jit(solution)/shard_map/dot_general | solution.py:33
  286.6 38.6 %all-gather.8.cloned.1.call-done.down = bf16[1024,2048]{1,0:T(8,128)(2,1)} async-done(((bf16[1024,512]{1,0:T(8,128)(2,1)}), bf16[1024,2048]{1,0:T(8,128)(2,1)}) %all-gather.8.cloned.1.call-update) | async-done | bytes 4194320 | tf_op jit(solution)/shard_map/all_gather | solution.py:1155
  325.3 16.0 %multiply_convert_fusion = (bf16[2048,1024]{1,0:T(8,128)(2,1)S(1)}, bf16[2048,1024]{1,0:T(8,128)(2,1)S(1)}) fusion(bf16[2048,1024]{1,0:T(8,128)(2,1)} %get-tuple-element.74, bf16[2048,1024]{1,0:T(8,128)(2,1)} %get-tuple-element.73, bf16[2048,2048]{1,0:T(8,128)(2,1)} %get-tuple-element.71, bf16[1024,2048]{1,0:T(8,128)(2,1)} %all-gather.8.cloned.1.call-done.down), kind=kOutput, calls=%fused_computation.1 | convolution fusion | flops 8602517504 | bytes 29360128 | tf_op jit(solution)/shard_map/dot_general | solution.py:37
  341.3 15.8 %convolution_convert_fusion.2 = bf16[2048,1024]{1,0:T(8,128)(2,1)} fusion(bf16[2048,2048]{1,0:T(8,128)(2,1)} %get-tuple-element.66, bf16[2048,1024]{1,0:T(8,128)(2,1)S(1)} %get-tuple-element.75.gate_hbm), kind=kOutput, calls=%fused_computation.10 | convolution fusion | flops 8592031744 | bytes 16777216 | tf_op jit(solution)/shard_map/dot_general | solution.py:33
  357.1 12.9 %convolution_convert_fusion.1 = bf16[2048,1024]{1,0:T(8,128)(2,1)} fusion(bf16[2048,2048]{1,0:T(8,128)(2,1)} %get-tuple-element.66, bf16[2048,1024]{1,0:T(8,128)(2,1)S(1)} %get-tuple-element.76.up_hbm), kind=kOutput, calls=%fused_computation.9 | convolution fusion | flops 8592031744 | bytes 16777216 | tf_op jit(solution)/shard_map/dot_general | solution.py:33
  370.0 8.4 %pad_maximum_fusion = bf16[2048,2048]{1,0:T(8,128)(2,1)} fusion(bf16[2048,1024]{1,0:T(8,128)(2,1)} %convolution_convert_fusion.1, bf16[2048,1024]{1,0:T(8,128)(2,1)} %convolution_convert_fusion.2), kind=kLoop, calls=%fused_computation | loop fusion | flops 16777216 | bytes 16777216 | tf_op jit(solution)/shard_map/concatenate | solution.py:1216
  378.4 0.0 reduce-scatter.8.cloned.1.call-start
  378.5 91.6 %shard_map.235 = (bf16[2048,2048]{1,0:T(8,128)(2,1)}, f32[256,2048]{1,0:T(8,128)}, f32[1,2048]{1,0:T(1,128)}) custom-call(bf16[2048,1024]{1,0:T(8,128)(2,1)} %copy-done.2, bf16[2048,1024]{1,0:T(8,128)(2,1)} %copy-done.1, bf16[2048,2048]{1,0:T(8,128)(2,1)} %all-gather.6.cloned.1.call-done.weights_hbm, f32[256,2048]{1,0:T(8,128)} %get-tuple-element.77.resid_hbm, ...), custom_call_target="tpu_custom_call" | custom-call | bytes 300000000 | tf_op jit(solution)/shard_map/pallas_call | solution.py:817
  470.1 7.4 %convolution_convert_fusion.5.cot_hbm = bf16[2048,256]{1,0:T(8,128)(2,1)} fusion(bf16[2048,2048]{1,0:T(8,128)(2,1)} %get-tuple-element.78, bf16[2048,1024]{1,0:T(8,128)(2,1)} %all-gather.4.cloned.1.call-done.weight.weights), kind=kOutput, calls=%fused_computation.15 | convolution fusion | flops 2148007936 | bytes 10485760 | tf_op jit(solution)/shard_map/dot_general | solution.py:29
  477.4 2.7 convolution_convert_fusion.4
  480.1 0.6 collective-permute-start
  480.7 65.4 %shard_map.236 = (bf16[2048,768]{1,0:T(8,128)(2,1)}, bf16[256,2048]{1,0:T(8,128)(2,1)}) custom-call(bf16[2048,768]{1,0:T(8,128)(2,1)} %get-tuple-element.63.rot_hbm, f32[2048,128]{1,0:T(8,128)} %copy.30.cos_ref.cos_hbm, f32[2048,128]{1,0:T(8,128)} %copy.31.sin_ref.sin_hbm, s32[2048,1]{1,0:T(8,128)} %copy.32.seg_col, s32[1,2048]{1,0:T(1,128)} %bitcast.64, ...), custom_call_target="tpu_custom_call" | custom-call | bytes 220000000 | tf_op jit(solution)/shard_map/pallas_call | solution.py:963
  546.2 10.6 %convolution_convert_fusion.3 = bf16[2048,768]{1,0:T(8,128)(2,1)S(1)} fusion(bf16[2048,2048]{1,0:T(8,128)(2,1)} %get-tuple-element.62, bf16[2048,768]{1,0:T(8,128)(2,1)} %get-tuple-element.89.cots), kind=kOutput, calls=%fused_computation.11 | convolution fusion | flops 6444023808 | bytes 14680064 | tf_op jit(solution)/shard_map/dot_general | solution.py:33
  556.8 2.6 pad_maximum_fusion.1
  559.5 1.3 collective-permute-start.3
  560.8 0.6 copy.45
  561.4 0.9 collective-permute-start.6
  562.3 82.4 %shard_map.238 = (bf16[256,2048]{1,0:T(8,128)(2,1)}, f32[2,2048]{1,0:T(2,128)}) custom-call(bf16[2048,768]{1,0:T(8,128)(2,1)} %get-tuple-element.89.cots, bf16[2048,1024]{1,0:T(8,128)(2,1)} %all-gather.4.cloned.1.call-done.weight.weights, f32[256,2048]{1,0:T(8,128)} %get-tuple-element.90.cot_hbm, bf16[512,2048]{1,0:T(8,128)(2,1)} %bitcast.53, ...), custom_call_target="tpu_custom_call" | custom-call | bytes 180000000 | tf_op jit(solution)/shard_map/pallas_call | solution.py:888
  644.7 0.1 collective-permute-start.4
  644.8 0.5 collective-permute-start.5
  645.3 0.1 collective-permute-start.1
  645.4 0.4 collective-permute-start.2
  645.8 0.8 collective-permute-start.7
  646.6 0.6 broadcast_xor_fusion.at
  647.1 6.4 collective-permute-done.1.refs_2_
  653.5 0.3 collective-permute-start.8
  653.9 4.7 maximum_select_fusion
  658.5 6.5 shard_map.237
  665.0 10.5 %shard_map.239 = (f32[512,4096]{1,0:T(8,128)}, f32[512,4096]{1,0:T(8,128)}) custom-call(s32[4]{0:T(128)} %broadcast_xor_fusion.at, bf16[512,2048]{1,0:T(8,128)(2,1)} %reduce-scatter.6.cloned.1.call-done.refs_0_, bf16[512,2048]{1,0:T(8,128)(2,1)} %collective-permute-done.3.refs_1_, bf16[512,2048]{1,0:T(8,128)(2,1)} %collective-permute-done.4.refs_2_, ...), custom_call_target="tpu_custom_call" | custom-call | bytes 25165824 | tf_op jit(solution)/shard_map/pallas_call | solution.py:1087
  675.5 0.5 collective-permute-start.9
  676.0 1.4 fusion.5
  677.4 1.7 collective-permute-done.8
  679.1 3.8 maximum_select_fusion.1
  682.8 1.0 copy-done.8
  683.8 6.6 shard_map.240
  (62 shorter events, 0.4 us)
Async XLA Ops:
  7.2 86.9 %all-gather.4.cloned.1.call-start = ((), (), s32[]{:S(2)}) async-start(), calls=%async_computation.3 | async-start | bytes 5242880 | tf_op jit(solution)/shard_map/all_gather | solution.py:1155
  9.6 4.6 copy-start.13
  9.7 5.2 copy-start.14
  9.7 5.2 copy-start.15
  9.7 234.4 %all-gather.6.cloned.1.call-start = ((), (), s32[]{:S(2)}) async-start(), calls=%async_computation.4 | async-start | bytes 10485760 | tf_op jit(solution)/shard_map/all_gather | solution.py:1155
  13.4 311.8 %all-gather.8.cloned.1.call-start = ((), (), s32[]{:S(2)}) async-start(), calls=%async_computation.5 | async-start | bytes 5242880 | tf_op jit(solution)/shard_map/all_gather | solution.py:1155
  14.2 466.0 %reduce-scatter.4.cloned.1.call-start = ((), (), s32[]{:S(2)}) async-start(), calls=%async_computation.6 | async-start | bytes 5242880 | tf_op jit(solution)/shard_map/reduce_scatter | solution.py:1158
  86.7 5.6 copy-start.10
  87.1 5.2 copy-start.12
  271.6 2.0 copy-start
  325.2 234.3 %reduce-scatter.6.cloned.1.call-start = ((), (), s32[]{:S(2)}) async-start(), calls=%async_computation.7 | async-start | bytes 10485760 | tf_op jit(solution)/shard_map/reduce_scatter | solution.py:1158
  341.3 15.9 %copy-start.2 = (bf16[2048,1024]{1,0:T(8,128)(2,1)}, bf16[2048,1024]{1,0:T(8,128)(2,1)S(1)}, u32[]{:S(2)}) copy-start(bf16[2048,1024]{1,0:T(8,128)(2,1)S(1)} %get-tuple-element.75.gate_hbm) | copy-start | bytes 12582916
  341.3 15.8 %copy-start.1 = (bf16[2048,1024]{1,0:T(8,128)(2,1)}, bf16[2048,1024]{1,0:T(8,128)(2,1)S(1)}, u32[]{:S(2)}) copy-start(bf16[2048,1024]{1,0:T(8,128)(2,1)S(1)} %get-tuple-element.76.up_hbm) | copy-start | bytes 12582916
  378.4 267.4 %reduce-scatter.8.cloned.1.call-start = ((), (), s32[]{:S(2)}) async-start(), calls=%async_computation.8 | async-start | bytes 5242880 | tf_op jit(solution)/shard_map/reduce_scatter | solution.py:1158
  470.1 7.4 %copy-start.9 = (bf16[2048,256]{1,0:T(8,128)(2,1)S(1)}, bf16[2048,256]{1,0:T(8,128)(2,1)}, u32[]{:S(2)}) copy-start(bf16[2048,256]{1,0:T(8,128)(2,1)} %get-tuple-element.64.mixed) | copy-start | bytes 3145732
  470.1 7.4 %copy-start.16 = (bf16[2048,2048]{1,0:T(8,128)(2,1)S(1)}, bf16[2048,2048]{1,0:T(8,128)(2,1)}, u32[]{:S(2)}) copy-start(bf16[2048,2048]{1,0:T(8,128)(2,1)} %get-tuple-element.78) | copy-start | bytes 25165828
  480.1 66.1 %collective-permute-start = (bf16[1024,512]{1,0:T(8,128)(2,1)}, bf16[1024,512]{1,0:T(8,128)(2,1)S(1)}, u32[]{:S(2)}, u32[]{:S(2)}) collective-permute-start(bf16[1024,512]{1,0:T(8,128)(2,1)} %reduce-scatter.4.cloned.1.call-done.refs_0_), channel_id=1, source_target_pairs={{0,4},{2,6},{4,0},{6,2},{1,5},{3,7},{5,1},{7,3},{8,12},{10,14},{12... | collective-permute-start | bytes 3145736 | tf_op jit(solution)/shard_map/ppermute | solution.py:292
  546.2 10.6 %copy-start.7 = (bf16[1024,512]{1,0:T(8,128)(2,1)}, bf16[1024,512]{1,0:T(8,128)(2,1)S(1)}, u32[]{:S(2)}) copy-start(bf16[1024,512]{1,0:T(8,128)(2,1)S(1)} %collective-permute-done.refs_1_) | copy-start | bytes 3145732
  559.4 1.4 copy-start.11
  559.5 85.2 %collective-permute-start.3 = (bf16[512,2048]{1,0:T(8,128)(2,1)}, bf16[512,2048]{1,0:T(8,128)(2,1)}, u32[]{:S(2)}, u32[]{:S(2)}) collective-permute-start(bf16[512,2048]{1,0:T(8,128)(2,1)} %reduce-scatter.6.cloned.1.call-done.refs_0_), channel_id=1, source_target_pairs={{0,4},{2,6},{4,0},{6,2},{1,5},{3,7},{5,1},{7,3},{8,12},{10,14},{12... | collective-permute-start | bytes 6291464 | tf_op jit(solution)/shard_map/ppermute | solution.py:292
  561.4 84.4 %collective-permute-start.6 = (bf16[256,2048]{1,0:T(8,128)(2,1)}, bf16[256,2048]{1,0:T(8,128)(2,1)}, u32[]{:S(2)}, u32[]{:S(2)}) collective-permute-start(bf16[256,2048]{1,0:T(8,128)(2,1)} %get-tuple-element.98), channel_id=1, source_target_pairs={{0,1},{1,0},{2,3},{3,2},{4,5},{5,4},{6,7},{7,6},{8,9},{9,8},{10,11... | collective-permute-start | bytes 3145736 | tf_op jit(solution)/shard_map/ppermute | solution.py:292
  562.3 82.4 %copy-start.3 = (bf16[512,2048]{1,0:T(8,128)(2,1)S(1)}, bf16[512,2048]{1,0:T(8,128)(2,1)}, u32[]{:S(2)}) copy-start(bf16[512,2048]{1,0:T(8,128)(2,1)} %reduce-scatter.6.cloned.1.call-done.refs_0_) | copy-start | bytes 6291460
  562.3 83.0 %copy-start.4 = (bf16[1024,512]{1,0:T(8,128)(2,1)S(1)}, bf16[1024,512]{1,0:T(8,128)(2,1)}, u32[]{:S(2)}) copy-start(bf16[1024,512]{1,0:T(8,128)(2,1)} %reduce-scatter.4.cloned.1.call-done.refs_0_) | copy-start | bytes 3145732
  562.3 84.3 %copy-start.17 = (s32[4]{0:T(128)S(1)}, s32[4]{0:T(128)}, u32[]{:S(2)}) copy-start(s32[4]{0:T(128)} %constant.34.clone) | copy-start | bytes 52
  644.7 20.3 %collective-permute-start.4 = (bf16[512,2048]{1,0:T(8,128)(2,1)S(1)}, bf16[512,2048]{1,0:T(8,128)(2,1)}, u32[]{:S(2)}, u32[]{:S(2)}) collective-permute-start(bf16[512,2048]{1,0:T(8,128)(2,1)S(1)} %copy-done.3), channel_id=1, source_target_pairs={{0,2},{2,0},{4,6},{6,4},{1,3},{3,1},{5,7},{7,5},{8,10},{10,8},{12,... | collective-permute-start | bytes 6291464 | tf_op jit(solution)/shard_map/ppermute | solution.py:292
  644.8 20.2 %collective-permute-start.5 = (bf16[512,2048]{1,0:T(8,128)(2,1)}, bf16[512,2048]{1,0:T(8,128)(2,1)}, u32[]{:S(2)}, u32[]{:S(2)}) collective-permute-start(bf16[512,2048]{1,0:T(8,128)(2,1)} %collective-permute-done.3.refs_1_), channel_id=1, source_target_pairs={{0,2},{2,0},{4,6},{6,4},{1,3},{3,1},{5,7},{7,5},{8,10},{10,8},{12,... | collective-permute-start | bytes 6291464 | tf_op jit(solution)/shard_map/ppermute | solution.py:292
  645.3 8.3 %collective-permute-start.1 = (bf16[1024,512]{1,0:T(8,128)(2,1)S(1)}, bf16[1024,512]{1,0:T(8,128)(2,1)}, u32[]{:S(2)}, u32[]{:S(2)}) collective-permute-start(bf16[1024,512]{1,0:T(8,128)(2,1)S(1)} %copy-done.4), channel_id=1, source_target_pairs={{0,2},{2,0},{4,6},{6,4},{1,3},{3,1},{5,7},{7,5},{8,10},{10,8},{12,... | collective-permute-start | bytes 3145736 | tf_op jit(solution)/shard_map/ppermute | solution.py:292
  645.4 13.2 %collective-permute-start.2 = (bf16[1024,512]{1,0:T(8,128)(2,1)}, bf16[1024,512]{1,0:T(8,128)(2,1)}, u32[]{:S(2)}, u32[]{:S(2)}) collective-permute-start(bf16[1024,512]{1,0:T(8,128)(2,1)} %copy-done.7), channel_id=1, source_target_pairs={{0,2},{2,0},{4,6},{6,4},{1,3},{3,1},{5,7},{7,5},{8,10},{10,8},{12,... | collective-permute-start | bytes 3145736 | tf_op jit(solution)/shard_map/ppermute | solution.py:292
  645.8 29.7 %collective-permute-start.7 = (bf16[512,1024]{1,0:T(8,128)(2,1)}, bf16[512,1024]{1,0:T(8,128)(2,1)}, u32[]{:S(2)}, u32[]{:S(2)}) collective-permute-start(bf16[512,1024]{1,0:T(8,128)(2,1)} %reduce-scatter.8.cloned.1.call-done.refs_0_), channel_id=1, source_target_pairs={{0,4},{2,6},{4,0},{6,2},{1,5},{3,7},{5,1},{7,3},{8,12},{10,14},{12... | collective-permute-start | bytes 3145736 | tf_op jit(solution)/shard_map/ppermute | solution.py:292
  653.5 25.5 %collective-permute-start.8 = (bf16[256,2048]{1,0:T(8,128)(2,1)}, bf16[256,2048]{1,0:T(8,128)(2,1)}, u32[]{:S(2)}, u32[]{:S(2)}) collective-permute-start(bf16[256,2048]{1,0:T(8,128)(2,1)} %get-tuple-element.100), channel_id=1, source_target_pairs={{0,1},{1,0},{2,3},{3,2},{4,5},{5,4},{6,7},{7,6},{8,9},{9,8},{10,11... | collective-permute-start | bytes 3145736 | tf_op jit(solution)/shard_map/ppermute | solution.py:292
  665.0 10.5 %copy-start.5 = (bf16[512,1024]{1,0:T(8,128)(2,1)S(1)}, bf16[512,1024]{1,0:T(8,128)(2,1)}, u32[]{:S(2)}) copy-start(bf16[512,1024]{1,0:T(8,128)(2,1)} %reduce-scatter.8.cloned.1.call-done.refs_0_) | copy-start | bytes 3145732
  665.0 14.1 %copy-start.6 = (bf16[256,2048]{1,0:T(8,128)(2,1)S(1)}, bf16[256,2048]{1,0:T(8,128)(2,1)}, u32[]{:S(2)}) copy-start(bf16[256,2048]{1,0:T(8,128)(2,1)} %get-tuple-element.100) | copy-start | bytes 3145732
  675.5 7.4 %collective-permute-start.10 = (bf16[512,1024]{1,0:T(8,128)(2,1)}, bf16[512,1024]{1,0:T(8,128)(2,1)S(1)}, u32[]{:S(2)}, u32[]{:S(2)}) collective-permute-start(bf16[512,1024]{1,0:T(8,128)(2,1)} %collective-permute-done.7.refs_1_), channel_id=1, source_target_pairs={{0,2},{2,0},{4,6},{6,4},{1,3},{3,1},{5,7},{7,5},{8,10},{10,8},{12,... | collective-permute-start | bytes 3145736 | tf_op jit(solution)/shard_map/ppermute | solution.py:292
  675.5 7.3 %collective-permute-start.9 = (bf16[512,1024]{1,0:T(8,128)(2,1)S(1)}, bf16[512,1024]{1,0:T(8,128)(2,1)}, u32[]{:S(2)}, u32[]{:S(2)}) collective-permute-start(bf16[512,1024]{1,0:T(8,128)(2,1)S(1)} %copy-done.5), channel_id=1, source_target_pairs={{0,2},{2,0},{4,6},{6,4},{1,3},{3,1},{5,7},{7,5},{8,10},{10,8},{12,... | collective-permute-start | bytes 3145736 | tf_op jit(solution)/shard_map/ppermute | solution.py:292
  682.8 1.0 copy-start.8
Sparse Core Ops, SparseCore 0:
  10.1 83.5 all-gather.3
  95.9 148.1 all-gather.5
  246.2 78.9 all-gather.7
  327.3 75.2 reduce-scatter.3
  405.4 145.1 reduce-scatter.5
  559.6 75.5 reduce-scatter.7
where the time goes:
time: 707 us; the launch traced here: 698 us
  Pallas kernels  453 us (64%)
  matrix products  112 us (16%)
  waiting for transfers between devices  72.2 us (10%)
  other arithmetic  28.2 us (4%)
  between operations  14.9 us (2%)
  local copies, waits for them, and re-layouts  12 us (2%)
    pallas_call x1, Pallas kernels, backward_mid(): pl.pallas_call(backward_mid_kernel, in_specs=[hbm] * 5 + [vmem], out_spec...  91.6 us
    pallas_call x1, Pallas kernels, forward_mid(): pl.pallas_call(forward_mid_kernel, in_specs=[vmem] * 4, out_specs=[pl.Blo...  84.8 us
    pallas_call x1, Pallas kernels, input_exchange(): pl.pallas_call(input_kernel, in_specs=[vmem] * 2 + [pl.BlockSpec(memory_s...  82.4 us
    pallas_call x1, Pallas kernels, start_exchange(): pl.pallas_call(start_kernel, in_specs=[vmem] * 4, out_specs=[hbm, hbm, vm...  70.5 us
    pallas_call x1, Pallas kernels, attention_output(): pl.pallas_call(attention_output_kernel, in_specs=[hbm] * 3 + [vmem] * 2 +...  65.4 us
    all_gather x3, waiting for transfers between devices, gather(): return lax.all_gather(weight, 'fsdp', axis=axis, tiled=True)  63.3 us
    dot_general x5, matrix products, contract_rows(): lax.dot_general(a, b, (((0,), (0,)), ((), ())), preferred_element_type=jn...  55 us
    dot_general x3, matrix products, product(): return jnp.dot(a, b, preferred_element_type=jnp.float32)  40.6 us
  transfers between devices with their start and end apart: 17, of which 4 were waited for; matrix products, arithmetic and copies ran while one was open for 21% of the time, Pallas kernels for 64%

commit v1 on v0

--- a/solution.py
+++ b/solution.py
@@ -351,6 +351,7 @@
 
 MESH = pl.DeviceIdType.MESH
 TILE = 512
+STEP = 32
 
 
 def fits_kernels():
@@ -366,6 +367,10 @@
         self.core = {"ctx": x * 2 + 1 - core}
         self.cross = {"ctx": (1 - x) * 2 + 1 - core}
         self.y = {"tp": 1 - self.tp}
+
+    def plane(self):
+        tp = self.y["tp"]
+        return [self.x, self.core, self.cross, self.y] + [dict(device, tp=tp) for device in (self.x, self.core, self.cross)]
 
     def others(self, axis):
         size, me = lax.axis_size(axis), lax.axis_index(axis)
@@ -707,7 +712,7 @@
     scatter.start()
     scatter.turn()
     scatter.finish()
-    step = 64
+    step = STEP
 
     def some(n, _):
         rows = aligned(n * step, step)
@@ -755,12 +760,12 @@
 
 
 def backward_mid_kernel(
-    gate_hbm, up_hbm, weights_hbm, resid_hbm, grads_hbm, gain, full, cot_out, gain_out,
-    gate_cot, up_cot, weights, resid, grads, sems, mine, *refs
+    hidden_hbm, weights_hbm, resid_hbm, grads_hbm, gain, full, cot_out, gain_out,
+    hidden_cot, weights, resid, grads, sems, mine, *refs
 ):
     place = Place()
     scatter_refs, (send, recv, local_sem) = refs[:-3], refs[-3:]
-    count, hidden_cols = gate_cot.shape
+    count = hidden_cot.shape[0]
     part = count // 8
     width = weights.shape[0]
     lower, upper = pl.ds(0, count // 2), pl.ds(count // 2, count // 2)
@@ -769,11 +774,9 @@
         sems,
         [
             (weights_hbm.at[left], weights.at[left]),
-            (gate_hbm.at[upper], gate_cot.at[upper]),
-            (up_hbm.at[upper], up_cot.at[upper]),
+            (hidden_hbm.at[upper], hidden_cot.at[upper]),
             (weights_hbm.at[right], weights.at[right]),
-            (gate_hbm.at[lower], gate_cot.at[lower]),
-            (up_hbm.at[lower], up_cot.at[lower]),
+            (hidden_hbm.at[lower], hidden_cot.at[lower]),
             (resid_hbm, resid),
             (grads_hbm.at[aligned(place.tp * part, part)], grads),
         ],
@@ -781,15 +784,15 @@
     meet([place.x, place.core, place.y])
 
     def make(rows, cols):
-        return contract_cols(gate_cot[rows, :], weights[cols, :hidden_cols]) + contract_cols(up_cot[rows, :], weights[cols, hidden_cols:])
+        return contract_cols(hidden_cot[rows, :], weights[cols, :])
 
     scatter = Scatter(place, make, count, scatter_refs)
-    scatter.start((loads[:3], loads[3:4], loads[4:6]))
+    scatter.start((loads[:2], loads[2:3], loads[3:4]))
     scatter.turn()
     scatter.finish()
-    for made in loads[6:]:
+    for made in loads[4:]:
         made.wait()
-    step = 32
+    step = STEP
 
     def some(n, sums):
         rows = aligned(n * step, step)
@@ -810,13 +813,13 @@
     stay.wait()
 
 
-def backward_mid(gate_cot, up_cot, weights, resid, grads, gain):
-    count, width = gate_cot.shape[0], weights.shape[0]
+def backward_mid(hidden_cot, weights, resid, grads, gain):
+    count, width = hidden_cot.shape[0], weights.shape[0]
     vmem = pl.BlockSpec(memory_space=pltpu.VMEM)
     hbm = pl.BlockSpec(memory_space=pl.ANY)
     return pl.pallas_call(
         backward_mid_kernel,
-        in_specs=[hbm] * 5 + [vmem],
+        in_specs=[hbm] * 4 + [vmem],
         out_specs=[pl.BlockSpec(memory_space=pl.ANY), vmem, vmem],
         out_shape=[
             jax.ShapeDtypeStruct((count, width), jnp.bfloat16),
@@ -824,17 +827,16 @@
             jax.ShapeDtypeStruct((1, width), jnp.float32),
         ],
         scratch_shapes=[
-            pltpu.VMEM(gate_cot.shape, jnp.bfloat16),
-            pltpu.VMEM(up_cot.shape, jnp.bfloat16),
+            pltpu.VMEM(hidden_cot.shape, jnp.bfloat16),
             pltpu.VMEM(weights.shape, jnp.bfloat16),
             pltpu.VMEM(resid.shape, jnp.float32),
             pltpu.VMEM(resid.shape, jnp.bfloat16),
-            pltpu.SemaphoreType.DMA((8,)),
+            pltpu.SemaphoreType.DMA((6,)),
         ]
         + mid_scratch(count, width),
         compiler_params=pltpu.CompilerParams(collective_id=2, has_side_effects=True, vmem_limit_bytes=VMEM_LIMIT),
         cost_estimate=pl.CostEstimate(flops=0, bytes_accessed=300_000_000, transcendentals=0),
-    )(gate_cot, up_cot, weights, resid, grads, gain[None, :])
+    )(hidden_cot, weights, resid, grads, gain[None, :])
 
 
 def input_kernel(cots, weights, cot_hbm, hidden_hbm, gain, gain_two, grad_out, gains_out, resid_cot, hidden, sems, sums, come, *refs):
@@ -843,7 +845,7 @@
     count = cots.shape[0]
     part = count // 8
     loads = load(sems, [(cot_hbm, resid_cot), (hidden_hbm.at[aligned(place.tp * part, part)], hidden)])
-    meet([place.x, place.core, place.y] + place.others("fsdp"))
+    meet(place.plane() + place.others("fsdp"))
     scatter = Scatter(place, lambda rows, cols: contract_cols(cots[rows, :], weights[cols, : cots.shape[1]]), count, refs, ("y", "y"))
     links = Links(send, recv)
     scatter.start()
@@ -851,7 +853,7 @@
     scatter.finish()
     for made in loads:
         made.wait()
-    step = 32
+    step = STEP
 
     def some(n, total):
         rows = aligned(n * step, step)
@@ -863,20 +865,16 @@
 
     sums[0, 0:1, :] = lax.fori_loop(0, part // step, some, jnp.zeros(gain.shape, jnp.float32))
     sums[0, 1:2, :] = gain_two[...]
-    near = [place.x, place.core, place.y]
-    for n, device in enumerate(near):
-        made = links.copy(sums.at[n], come.at[n], device)
-        made.start()
-        made.wait_recv()
-        sums[n + 1] = sums[n] + come[n]
-    at = len(near)
-    far = [links.copy(sums.at[at], come.at[at + n], device) for n, device in enumerate(place.others("fsdp"))]
-    for made in far:
-        made.start()
-    total = sums[at]
-    for n, made in enumerate(far):
-        made.wait_recv()
-        total = total + come[at + n]
+    total = sums[0]
+    for stage, devices in enumerate((place.plane(), place.others("fsdp"))):
+        at = stage * len(place.plane())
+        made = [links.copy(sums.at[stage], come.at[at + n], device) for n, device in enumerate(devices)]
+        for copy in made:
+            copy.start()
+        for n, copy in enumerate(made):
+            copy.wait_recv()
+            total = total + come[at + n]
+        sums[stage + 1] = total
     gains_out[...] = total
     links.drain()
 
@@ -894,11 +892,11 @@
             pltpu.VMEM(resid_cot.shape, jnp.float32),
             pltpu.VMEM(resid_cot.shape, jnp.bfloat16),
             pltpu.SemaphoreType.DMA((2,)),
-            pltpu.VMEM((4, 2, width), jnp.float32),
-            pltpu.VMEM((2 + fsdp, 2, width), jnp.float32),
+            pltpu.VMEM((3, 2, width), jnp.float32),
+            pltpu.VMEM((6 + fsdp, 2, width), jnp.float32),
         ]
         + scatter_scratch(count, width)
-        + [pltpu.SemaphoreType.DMA((4 + fsdp,)), pltpu.SemaphoreType.DMA((4 + fsdp,))],
+        + [pltpu.SemaphoreType.DMA((6 + fsdp,)), pltpu.SemaphoreType.DMA((6 + fsdp,))],
         compiler_params=pltpu.CompilerParams(collective_id=3, has_side_effects=True, vmem_limit_bytes=VMEM_LIMIT),
         cost_estimate=pl.CostEstimate(flops=0, bytes_accessed=180_000_000, transcendentals=0),
     )(cots, weights, resid_cot, hidden, gain[None, :], gain_two)
@@ -980,6 +978,35 @@
     )(rot, cos, sin, seg_col, seg_row, cot, mixed, lse, hidden_act, down, resid)
 
 
+def hidden_cot_kernel(cot, down, gate_slope, up_slope, out):
+    cols = down.shape[0]
+
+    def some(n, _):
+        at = aligned(n * TILE, TILE)
+        back = contract_cols(cot[...], down[at, :])
+        out[:, at] = low(back * gate_slope[:, at])
+        out[:, aligned(cols + n * TILE, TILE)] = low(back * up_slope[:, at])
+        return 0
+
+    lax.fori_loop(0, cols // TILE, some, 0)
+
+
+def hidden_cots(cot, down, gate_slope, up_slope):
+    count, width = cot.shape
+    cols = down.shape[0]
+    rows = 512
+    side = pl.BlockSpec((rows, cols), lambda n: (n, 0))
+    return pl.pallas_call(
+        hidden_cot_kernel,
+        grid=(count // rows,),
+        in_specs=[pl.BlockSpec((rows, width), lambda n: (n, 0)), pl.BlockSpec((cols, width), lambda n: (0, 0)), side, side],
+        out_specs=pl.BlockSpec((rows, 2 * cols), lambda n: (n, 0)),
+        out_shape=jax.ShapeDtypeStruct((count, 2 * cols), jnp.bfloat16),
+        compiler_params=pltpu.CompilerParams(vmem_limit_bytes=VMEM_LIMIT),
+        cost_estimate=pl.CostEstimate(flops=2 * count * width * cols, bytes_accessed=2 * count * (width + 4 * cols), transcendentals=0),
+    )(cot, down, gate_slope, up_slope)
+
+
 def take_attention_kernel(at, query, key, value, out, taken):
     pairs = query.shape[1] // PAIR
     for p in range(pairs):
@@ -1067,6 +1094,34 @@
         compiler_params=pltpu.CompilerParams(vmem_limit_bytes=VMEM_LIMIT),
         cost_estimate=pl.CostEstimate(flops=0, bytes_accessed=6 * math.prod(shape), transcendentals=0),
     )(order_of_pieces(), *pieces)
+
+
+def join_kernel(at, *refs):
+    outs = refs[-2:]
+    for n in range(2):
+
+        @pl.when(pl.program_id(0) == n)
+        def _():
+            for m, out in enumerate(outs):
+                out[...] = refs[2 * m + n][...]
+
+
+def join_rows(first, second):
+    rows, width = first[0].shape
+    me = lax.axis_index("tp")
+    whole = pl.BlockSpec((rows, width), lambda n, at: (0, 0))
+    return pl.pallas_call(
+        join_kernel,
+        grid_spec=pltpu.PrefetchScalarGridSpec(
+            num_scalar_prefetch=1,
+            grid=(2,),
+            in_specs=[whole] * 4,
+            out_specs=[pl.BlockSpec((rows, width), lambda n, at: (at[n], 0))] * 2,
+        ),
+        out_shape=[jax.ShapeDtypeStruct((2 * rows, width), first[0].dtype)] * 2,
+        compiler_params=pltpu.CompilerParams(vmem_limit_bytes=VMEM_LIMIT),
+        cost_estimate=pl.CostEstimate(flops=0, bytes_accessed=16 * rows * width, transcendentals=0),
+    )(jnp.stack([me, 1 - me]), *first, *second)
 
 
 def place_gate_up_kernel(at, *refs):
@@ -1210,20 +1265,14 @@
     down_part, full_down, branch_cot = lax.optimization_barrier((down_part, full_down, branch_cot))
     down_own = settle(down_part, 1)
 
-    hidden_cot = contract_cols(branch_cot, full_down)
-    gate_cot = low(hidden_cot * gate_slope)
-    up_cot = low(hidden_cot * up_slope)
-    gate_up_part = jnp.concatenate([low(contract_rows(mlp_in, gate_cot)), low(contract_rows(mlp_in, up_cot))], axis=1)
+    hidden_cot = hidden_cots(branch_cot, full_down, gate_slope, up_slope)
+    gate_up_part = low(contract_rows(mlp_in, hidden_cot))
     gate_up_own = settle(gate_up_part, 0)
     if kernels:
-        gate_cot, up_cot, gate_up_part = lax.optimization_barrier((gate_cot, up_cot, gate_up_part))
-        attn_cot, resid_cot, gain_two_part = backward_mid(gate_cot, up_cot, full_gate_up, resid, out_grad[0], gain_two)
+        hidden_cot, gate_up_part = lax.optimization_barrier((hidden_cot, gate_up_part))
+        attn_cot, resid_cot, gain_two_part = backward_mid(hidden_cot, full_gate_up, resid, out_grad[0], gain_two)
     else:
-        mlp_in_cot = scatter_both(
-            lambda lo, hi: contract_cols(gate_cot[lo:hi], full_gate_up[:, :ff_cols])
-            + contract_cols(up_cot[lo:hi], full_gate_up[:, ff_cols:]),
-            tokens,
-        )
+        mlp_in_cot = scatter_both(lambda lo, hi: contract_cols(hidden_cot[lo:hi], full_gate_up), tokens)
         back, terms = norm_back(resid, r2, gain_two, mlp_in_cot)
         gain_two_part = jnp.sum(terms, axis=0, keepdims=True)
         resid_cot = wide(own_part(out_grad[0])) + back
@@ -1234,7 +1283,7 @@
     down_pieces = first_swaps(down_own)
     if kernels:
         cots, output = attention_output(rot, cos, sin, seg_col, seg_row, mixed_cot, mixed_wide, lse, hidden, full_down, resid)
-        output = join_tp(output)
+        other_output = swap(output, "tp", 1)
     else:
         cots = attention_backward(info, rot, cos, sin, seg_col, seg_row, mixed_cot, mixed_wide, lse)
     cots, *down_pieces = lax.optimization_barrier((cots, *down_pieces))
@@ -1246,7 +1295,8 @@
         gate_up_pieces = first_swaps(gate_up_own)
         input_grad, gain_sums = input_exchange(cots, w_attn, resid_cot, hidden_in[0], gain_one, gain_two_part)
         input_grad, *gate_up_pieces = lax.optimization_barrier((input_grad, *gate_up_pieces))
-        input_grad = join_tp(input_grad)
+        other_input = swap(input_grad, "tp", 1)
+        output, input_grad = join_rows((output, other_output), (input_grad, other_input))
     else:
         gate_up_pieces = first_swaps(gate_up_own)
         out_sum = scatter_both(lambda lo, hi: product(hidden[lo:hi], full_down), tokens)
@@ -1256,11 +1306,11 @@
         input_grad = join_tp(low(resid_cot + back))
         gain_sums = lax.psum(jnp.concatenate([jnp.sum(terms, axis=0, keepdims=True), gain_two_part]), ("fsdp", "ctx", "tp"))
     attn_pieces = first_swaps(attn_own)
-    down_grad = place_pieces(last_swap(down_pieces), 0)
-    gate_grad, up_grad = place_gate_up(last_swap(gate_up_pieces))
-    down_grad, gate_grad, up_grad, output, *attn_pieces = lax.optimization_barrier(
-        (down_grad, gate_grad, up_grad, output, *attn_pieces)
-    )
+    down_pieces = last_swap(down_pieces)
+    down_grad = place_pieces(down_pieces, 0)
+    gate_up_pieces = last_swap(gate_up_pieces)
+    gate_grad, up_grad = place_gate_up(gate_up_pieces)
+    down_grad, gate_grad, up_grad, *attn_pieces = lax.optimization_barrier((down_grad, gate_grad, up_grad, *attn_pieces))
     query_grad, key_grad, value_grad, out_proj_grad = place_attention(last_swap(attn_pieces))
 
     gain_sums = lax.dynamic_slice_in_dim(gain_sums, lax.axis_index("fsdp") * attn_gain.shape[0], attn_gain.shape[0], 1)

time: 707 us -> 719 us (1.017)
  waiting for transfers between devices: 72.2 us -> 102 us
  matrix products: 112 us -> 90.8 us
  Pallas kernels: 453 us -> 473 us
  other arithmetic: 28.2 us -> 12 us
    ppermute x11, waiting for transfers between devices: 8.1 us -> 33.9 us  [swap(): return lax.ppermute(values, axis, [(i, i ^ mask) for i in range(size)])]
    pallas_call x1 -> x3, Pallas kernels: 91.6 us -> 113 us  [the longest x1 91.4 us: backward_mid(): pl.pallas_call(backward_mid_kernel, in_specs=[hbm] * 4 + [vmem], out_spec...]
    dot_general x1 -> x0, matrix products: 16 us -> none  [contract_cols(): lax.dot_general(a, b, (((1,), (1,)), ((), ())), preferred_element_type=jn...]
    select_n x2 -> x0, other arithmetic: 8.43 us -> none  [join_tp(): jnp.where(upper, jnp.concatenate([other, rows], 0), jnp.concatenate([rows...]
    concatenate x1 -> x0, other arithmetic: 8.41 us -> none  [local(): jnp.concatenate([low(contract_rows(mlp_in, gate_cot)), low(contract_rows(...]
    dot_general x5 -> x4, matrix products: 55 us -> 50 us  [contract_rows(): lax.dot_general(a, b, (((0,), (0,)), ((), ())), preferred_element_type=jn...]
  transfers between devices with their start and end apart: 17 -> 17, of which waited for: 4 -> 7; matrix products, arithmetic and copies ran while one was open for 21% -> 16% of each run, Pallas kernels for 64% -> 65%
where the time goes in v1:
time: 719 us; the launch traced here: 710 us
  Pallas kernels  473 us (66%)
  waiting for transfers between devices  102 us (14%)
  matrix products  90.8 us (13%)
  between operations  14.6 us (2%)
  local copies, waits for them, and re-layouts  12 us (2%)
  other arithmetic  12 us (2%)
    pallas_call x1, Pallas kernels, backward_mid(): pl.pallas_call(backward_mid_kernel, in_specs=[hbm] * 4 + [vmem], out_spec...  91.4 us
    pallas_call x1, Pallas kernels, forward_mid(): pl.pallas_call(forward_mid_kernel, in_specs=[vmem] * 4, out_specs=[pl.Blo...  85.2 us
    pallas_call x1, Pallas kernels, input_exchange(): pl.pallas_call(input_kernel, in_specs=[vmem] * 2 + [pl.BlockSpec(memory_s...  81.1 us
    pallas_call x1, Pallas kernels, start_exchange(): pl.pallas_call(start_kernel, in_specs=[vmem] * 4, out_specs=[hbm, hbm, vm...  70.5 us
    pallas_call x1, Pallas kernels, attention_output(): pl.pallas_call(attention_output_kernel, in_specs=[hbm] * 3 + [vmem] * 2 +...  65 us
    all_gather x3, waiting for transfers between devices, gather(): return lax.all_gather(weight, 'fsdp', axis=axis, tiled=True)  62.1 us
    dot_general x4, matrix products, contract_rows(): lax.dot_general(a, b, (((0,), (0,)), ((), ())), preferred_element_type=jn...  50 us
    dot_general x3, matrix products, product(): return jnp.dot(a, b, preferred_element_type=jnp.float32)  40.8 us
  transfers between devices with their start and end apart: 17, of which 7 were waited for; matrix products, arithmetic and copies ran while one was open for 16% of the time, Pallas kernels for 65%

profile of v1, /device:TPU:0, one launch (start us, length us, event | category | flops | bytes accessed | tf_op | source)
XLA Modules:
  0.0 709.6 jit_solution(14888482155435658917)
XLA Ops:
  7.2 2.4 shard_map.231
  9.7 3.7 shard_map.234
  13.5 0.7 all-gather.8.cloned.1.call-update
  14.2 0.6 concatenate.14.segs
  14.8 0.6 maximum_convert_fusion.gains
  15.4 70.5 %shard_map.230 = (bf16[2048,2048]{1,0:T(8,128)(2,1)}, bf16[2048,2048]{1,0:T(8,128)(2,1)}, s32[4,8,128]{2,1,0:T(8,128)}, f32[4,8,128]{2,1,0:T(8,128)}) custom-call(bf16[512,2048]{1,0:T(8,128)(2,1)} %bitcast.48, bf16[512,2048]{1,0:T(8,128)(2,1)} %bitcast.51, s32[8,128]{1,0:T(8,128)} %concatenate.14.segs, f32[8,128]{1,0:T(8,128)} %maximum_convert_fusion.gains), custom_call_target="tpu_custom_call" | custom-call | bytes 200000000 | tf_op jit(solution)/shard_map/pallas_call | solution.py:512
  86.0 0.7 slice.43
  86.7 0.1 slice.44
  86.8 0.1 slice.45
  86.9 0.1 pad_add_fusion.2
  86.9 0.1 add_bitcast_fusion
  87.0 0.1 slice.42
  87.1 1.0 multiply_sine_fusion
  88.1 0.1 tile.8
  88.2 1.3 copy.28.cos_ref.cos_hbm
  89.5 0.1 tile.20
  89.7 1.3 copy.29.sin_ref.sin_hbm
  91.0 1.3 copy.30.seg_col
  92.3 0.6 slice_bitcast_fusion
  92.9 0.6 copy.38
  93.5 0.6 pad_add_fusion.info
  94.1 11.7 %fusion.1.qkv_ref = f32[2048,768]{1,0:T(8,128)} fusion(bf16[2048,2048]{1,0:T(8,128)(2,1)} %get-tuple-element.62, bf16[2048,1024]{1,0:T(8,128)(2,1)} %all-gather.4.cloned.1.call-done.weight.weights), kind=kOutput, calls=%fused_computation.8 | convolution fusion | flops 6442450944 | bytes 17825792 | tf_op jit(solution)/shard_map/dot_general | solution.py:29
  105.8 28.7 %shard_map.232 = (bf16[2048,768]{1,0:T(8,128)(2,1)}, bf16[2048,256]{1,0:T(8,128)(2,1)}, f32[2048,256]{1,0:T(8,128)}, f32[2,2,2048]{2,1,0:T(2,128)}) custom-call(s32[3,4]{1,0:T(4,128)} %pad_add_fusion.info, f32[2048,768]{1,0:T(8,128)} %fusion.1.qkv_ref, f32[2048,128]{1,0:T(8,128)} %copy.28.cos_ref.cos_hbm, f32[2048,128]{1,0:T(8,128)} %copy.29.sin_ref.sin_hbm, ...), custom_call_target="tpu_custom_call" | custom-call | flops 3221225472 | bytes 15728640 | tf_op jit(solution)/shard_map/pallas_call | solution.py:224
  134.5 85.2 %shard_map.233 = (bf16[2048,2048]{1,0:T(8,128)(2,1)}, f32[256,2048]{1,0:T(8,128)}) custom-call(bf16[2048,256]{1,0:T(8,128)(2,1)} %get-tuple-element.64.mixed, bf16[2048,1024]{1,0:T(8,128)(2,1)} %all-gather.4.cloned.1.call-done.weight.weights, bf16[512,2048]{1,0:T(8,128)(2,1)} %bitcast.49, f32[1,2048]{1,0:T(1,128)} %bitcast.60), custom_call_target="tpu_custom_call" | custom-call | bytes 300000000 | tf_op jit(solution)/shard_map/pallas_call | solution.py:745
  219.7 24.4 %all-gather.6.cloned.1.call-done.weights_hbm = bf16[2048,2048]{1,0:T(8,128)(2,1)} async-done(((bf16[512,2048]{1,0:T(8,128)(2,1)}), bf16[2048,2048]{1,0:T(8,128)(2,1)}) %all-gather.6.cloned.1.call-update) | async-done | bytes 8388624 | tf_op jit(solution)/shard_map/all_gather | solution.py:1210
  244.1 21.9 %fusion.6 = f32[2048,2048]{1,0:T(8,128)S(1)} fusion(bf16[2048,2048]{1,0:T(8,128)(2,1)} %get-tuple-element.66, bf16[2048,2048]{1,0:T(8,128)(2,1)} %all-gather.6.cloned.1.call-done.weights_hbm), kind=kOutput, calls=%fused_computation.28 | convolution fusion | flops 17179869184 | bytes 33554432 | tf_op jit(solution)/shard_map/dot_general | solution.py:29
  266.0 5.9 fusion.4
  271.9 2.0 copy-done
  273.9 13.1 %convolution_convert_fusion.1 = bf16[1024,2048]{1,0:T(8,128)(2,1)} fusion(bf16[2048,1024]{1,0:T(8,128)(2,1)S(1)} %get-tuple-element.68.hidden_act, bf16[2048,2048]{1,0:T(8,128)(2,1)} %get-tuple-element.71.cot), kind=kOutput, calls=%fused_computation.6 | convolution fusion | flops 8592031744 | bytes 16777216 | tf_op jit(solution)/shard_map/dot_general | solution.py:33
  286.9 37.7 %all-gather.8.cloned.1.call-done.down = bf16[1024,2048]{1,0:T(8,128)(2,1)} async-done(((bf16[1024,512]{1,0:T(8,128)(2,1)}), bf16[1024,2048]{1,0:T(8,128)(2,1)}) %all-gather.8.cloned.1.call-update) | async-done | bytes 4194320 | tf_op jit(solution)/shard_map/all_gather | solution.py:1210
  324.7 16.3 %shard_map.235.hidden_hbm = bf16[2048,2048]{1,0:T(8,128)(2,1)} custom-call(bf16[2048,2048]{1,0:T(8,128)(2,1)} %get-tuple-element.71.cot, bf16[1024,2048]{1,0:T(8,128)(2,1)} %all-gather.8.cloned.1.call-done.down, bf16[2048,1024]{1,0:T(8,128)(2,1)} %get-tuple-element.73.gate_slope, bf16[2048,1024]{1,0:T(8,128)(2,1)} %get-tuple-element.74.up_slope), custom_call_target="tpu_custom_call" | custom-call | flops 8589934592 | bytes 25165824 | tf_op jit(solution)/shard_map/pallas_call | solution.py:999
  341.0 23.7 %convolution_convert_fusion = bf16[2048,2048]{1,0:T(8,128)(2,1)} fusion(bf16[2048,2048]{1,0:T(8,128)(2,1)} %get-tuple-element.66, bf16[2048,2048]{1,0:T(8,128)(2,1)} %shard_map.235.hidden_hbm), kind=kOutput, calls=%fused_computation.4 | convolution fusion | flops 17184063488 | bytes 25165824 | tf_op jit(solution)/shard_map/dot_general | solution.py:33
  364.7 0.0 reduce-scatter.8.cloned.1.call-start
  364.8 91.4 %shard_map.236 = (bf16[2048,2048]{1,0:T(8,128)(2,1)}, f32[256,2048]{1,0:T(8,128)}, f32[1,2048]{1,0:T(1,128)}) custom-call(bf16[2048,2048]{1,0:T(8,128)(2,1)} %shard_map.235.hidden_hbm, bf16[2048,2048]{1,0:T(8,128)(2,1)} %all-gather.6.cloned.1.call-done.weights_hbm, f32[256,2048]{1,0:T(8,128)} %get-tuple-element.76.resid_hbm, bf16[512,2048]{1,0:T(8,128)(2,1)} %bitcast.52, ...), custom_call_target="tpu_custom_call" | custom-call | bytes 300000000 | tf_op jit(solution)/shard_map/pallas_call | solution.py:820
  456.2 7.2 %convolution_convert_fusion.4.cot_hbm = bf16[2048,256]{1,0:T(8,128)(2,1)} fusion(bf16[2048,2048]{1,0:T(8,128)(2,1)} %get-tuple-element.77, bf16[2048,1024]{1,0:T(8,128)(2,1)} %all-gather.4.cloned.1.call-done.weight.weights), kind=kOutput, calls=%fused_computation.11 | convolution fusion | flops 2148007936 | bytes 10485760 | tf_op jit(solution)/shard_map/dot_general | solution.py:29
  463.4 2.7 convolution_convert_fusion.3
  466.1 0.6 collective-permute-start.1
  466.7 65.0 %shard_map.237 = (bf16[2048,768]{1,0:T(8,128)(2,1)}, bf16[256,2048]{1,0:T(8,128)(2,1)}) custom-call(bf16[2048,768]{1,0:T(8,128)(2,1)} %get-tuple-element.63.rot_hbm, f32[2048,128]{1,0:T(8,128)} %copy.28.cos_ref.cos_hbm, f32[2048,128]{1,0:T(8,128)} %copy.29.sin_ref.sin_hbm, s32[2048,1]{1,0:T(8,128)} %copy.30.seg_col, s32[1,2048]{1,0:T(1,128)} %bitcast.59, ...), custom_call_target="tpu_custom_call" | custom-call | bytes 220000000 | tf_op jit(solution)/shard_map/pallas_call | solution.py:961
  531.7 10.7 %convolution_convert_fusion.2 = bf16[2048,768]{1,0:T(8,128)(2,1)S(1)} fusion(bf16[2048,2048]{1,0:T(8,128)(2,1)} %get-tuple-element.62, bf16[2048,768]{1,0:T(8,128)(2,1)} %get-tuple-element.87.cots), kind=kOutput, calls=%fused_computation.7 | convolution fusion | flops 6444023808 | bytes 14680064 | tf_op jit(solution)/shard_map/dot_general | solution.py:33
  542.4 2.6 pad_maximum_fusion
  545.1 5.0 reduce-scatter.6.cloned.1.call-done.refs_0_
  550.1 1.5 collective-permute-start.2
  551.5 0.6 copy.39
  552.1 81.1 %shard_map.238 = (bf16[256,2048]{1,0:T(8,128)(2,1)}, f32[2,2048]{1,0:T(2,128)}) custom-call(bf16[2048,768]{1,0:T(8,128)(2,1)} %get-tuple-element.87.cots, bf16[2048,1024]{1,0:T(8,128)(2,1)} %all-gather.4.cloned.1.call-done.weight.weights, f32[256,2048]{1,0:T(8,128)} %get-tuple-element.88.cot_hbm, bf16[512,2048]{1,0:T(8,128)(2,1)} %bitcast.50, ...), custom_call_target="tpu_custom_call" | custom-call | bytes 180000000 | tf_op jit(solution)/shard_map/pallas_call | solution.py:886
  633.3 0.1 collective-permute-start.6
  633.3 0.5 collective-permute-start.7
  633.8 0.1 collective-permute-start.4
  633.9 0.4 collective-permute-start.5
  634.3 0.6 collective-permute-start.8
  634.9 0.6 broadcast_xor_fusion.at
  635.5 6.6 collective-permute-done.4.refs_2_
  642.1 0.5 collective-permute-start
  642.6 1.0 collective-permute-done.5.refs_3_
  643.6 6.5 shard_map.240
  650.1 0.5 collective-permute-start.3
  650.6 10.5 %shard_map.241 = (f32[512,4096]{1,0:T(8,128)}, f32[512,4096]{1,0:T(8,128)}) custom-call(s32[4]{0:T(128)} %broadcast_xor_fusion.at, bf16[512,2048]{1,0:T(8,128)(2,1)} %reduce-scatter.6.cloned.1.call-done.refs_0_, bf16[512,2048]{1,0:T(8,128)(2,1)} %collective-permute-done.2.refs_1_, bf16[512,2048]{1,0:T(8,128)(2,1)} %collective-permute-done.6.refs_2_, ...), custom_call_target="tpu_custom_call" | custom-call | bytes 25165824 | tf_op jit(solution)/shard_map/pallas_call | solution.py:1142
  661.1 0.5 collective-permute-start.9
  661.6 0.6 pad_add_fusion.1.at
  662.2 1.4 fusion.5
  663.6 4.6 collective-permute-done.refs_1_
  668.3 21.6 %collective-permute-done.3.refs_3_ = bf16[256,2048]{1,0:T(8,128)(2,1)} collective-permute-done((bf16[256,2048]{1,0:T(8,128)(2,1)}, bf16[256,2048]{1,0:T(8,128)(2,1)}, u32[]{:S(2)}, u32[]{:S(2)}) %collective-permute-start.3) | collective-permute-done | bytes 1048608 | tf_op jit(solution)/shard_map/ppermute | solution.py:292
  689.9 5.0 shard_map.239
  694.9 1.0 copy-done.5
  695.9 6.6 shard_map.242
  (57 shorter events, 0.4 us)
Async XLA Ops:
  7.2 87.0 %all-gather.4.cloned.1.call-start = ((), (), s32[]{:S(2)}) async-start(), calls=%async_computation.3 | async-start | bytes 5242880 | tf_op jit(solution)/shard_map/all_gather | solution.py:1210
  9.6 4.6 copy-start.10
  9.6 5.2 copy-start.11
  9.6 5.2 copy-start.12
  9.7 234.4 %all-gather.6.cloned.1.call-start = ((), (), s32[]{:S(2)}) async-start(), calls=%async_computation.4 | async-start | bytes 10485760 | tf_op jit(solution)/shard_map/all_gather | solution.py:1210
  13.4 311.2 %all-gather.8.cloned.1.call-start = ((), (), s32[]{:S(2)}) async-start(), calls=%async_computation.5 | async-start | bytes 5242880 | tf_op jit(solution)/shard_map/all_gather | solution.py:1210
  14.2 451.9 %reduce-scatter.4.cloned.1.call-start = ((), (), s32[]{:S(2)}) async-start(), calls=%async_computation.6 | async-start | bytes 5242880 | tf_op jit(solution)/shard_map/reduce_scatter | solution.py:1213
  86.0 6.4 copy-start.9
  86.7 19.1 %copy-start.7 = (s32[4,4,128]{2,1,0:T(4,128)}, s32[4,4,128]{2,1,0:T(4,128)S(1)}, u32[]{:S(2)}) copy-start(s32[4,4,128]{2,1,0:T(4,128)S(1)} %slice.43) | copy-start | bytes 24580
  271.9 2.0 copy-start
  324.7 225.4 %reduce-scatter.6.cloned.1.call-start = ((), (), s32[]{:S(2)}) async-start(), calls=%async_computation.7 | async-start | bytes 10485760 | tf_op jit(solution)/shard_map/reduce_scatter | solution.py:1213
  364.7 269.6 %reduce-scatter.8.cloned.1.call-start = ((), (), s32[]{:S(2)}) async-start(), calls=%async_computation.8 | async-start | bytes 5242880 | tf_op jit(solution)/shard_map/reduce_scatter | solution.py:1213
  456.2 7.2 %copy-start.6 = (bf16[2048,256]{1,0:T(8,128)(2,1)S(1)}, bf16[2048,256]{1,0:T(8,128)(2,1)}, u32[]{:S(2)}) copy-start(bf16[2048,256]{1,0:T(8,128)(2,1)} %get-tuple-element.64.mixed) | copy-start | bytes 3145732
  456.2 7.2 %slice-start = ((s8[8388608]{0:T(1024)(128)(4,1)}), s8[4194304]{0:T(1024)(128)(4,1)S(1)}, s32[]{:S(2)}) async-start(s8[8388608]{0:T(1024)(128)(4,1)} %bitcast.74), calls=%async_computation.9 | async-start | bytes 8388608
  456.2 7.2 %slice-start.1 = ((s8[8388608]{0:T(1024)(128)(4,1)}), s8[4194304]{0:T(1024)(128)(4,1)S(1)}, s32[]{:S(2)}) async-start(s8[8388608]{0:T(1024)(128)(4,1)} %bitcast.74), calls=%async_computation.10 | async-start | bytes 8388608
  466.1 65.6 %collective-permute-start.1 = (bf16[1024,512]{1,0:T(8,128)(2,1)}, bf16[1024,512]{1,0:T(8,128)(2,1)S(1)}, u32[]{:S(2)}, u32[]{:S(2)}) collective-permute-start(bf16[1024,512]{1,0:T(8,128)(2,1)} %reduce-scatter.4.cloned.1.call-done.refs_0_), channel_id=1, source_target_pairs={{0,4},{2,6},{4,0},{6,2},{1,5},{3,7},{5,1},{7,3},{8,12},{10,14},{12... | collective-permute-start | bytes 3145736 | tf_op jit(solution)/shard_map/ppermute | solution.py:292
  531.7 10.7 %copy-start.4 = (bf16[1024,512]{1,0:T(8,128)(2,1)}, bf16[1024,512]{1,0:T(8,128)(2,1)S(1)}, u32[]{:S(2)}) copy-start(bf16[1024,512]{1,0:T(8,128)(2,1)S(1)} %collective-permute-done.1.refs_1_) | copy-start | bytes 3145732
  542.4 9.1 %copy-start.8 = (f32[1,1,4,512]{3,2,1,0:T(4,128)S(1)}, f32[1,1,4,512]{3,2,1,0:T(4,128)}, u32[]{:S(2)}) copy-start(f32[1,1,4,512]{3,2,1,0:T(4,128)} %get-tuple-element.116) | copy-start | bytes 24580
  545.0 89.9 %copy-start.13 = (s32[4]{0:T(128)S(1)}, s32[4]{0:T(128)}, u32[]{:S(2)}) copy-start(s32[4]{0:T(128)} %constant.34.clone) | copy-start | bytes 52
  545.0 97.1 %copy-start.2 = (bf16[256,2048]{1,0:T(8,128)(2,1)S(1)}, bf16[256,2048]{1,0:T(8,128)(2,1)}, u32[]{:S(2)}) copy-start(bf16[256,2048]{1,0:T(8,128)(2,1)} %get-tuple-element.82.refs_0_) | copy-start | bytes 3145732
  550.0 83.2 %copy-start.1 = (bf16[512,2048]{1,0:T(8,128)(2,1)S(1)}, bf16[512,2048]{1,0:T(8,128)(2,1)}, u32[]{:S(2)}) copy-start(bf16[512,2048]{1,0:T(8,128)(2,1)} %reduce-scatter.6.cloned.1.call-done.refs_0_) | copy-start | bytes 6291460
  550.1 83.2 %collective-permute-start.2 = (bf16[512,2048]{1,0:T(8,128)(2,1)}, bf16[512,2048]{1,0:T(8,128)(2,1)}, u32[]{:S(2)}, u32[]{:S(2)}) collective-permute-start(bf16[512,2048]{1,0:T(8,128)(2,1)} %reduce-scatter.6.cloned.1.call-done.refs_0_), channel_id=1, source_target_pairs={{0,4},{2,6},{4,0},{6,2},{1,5},{3,7},{5,1},{7,3},{8,12},{10,14},{12... | collective-permute-start | bytes 6291464 | tf_op jit(solution)/shard_map/ppermute | solution.py:292
  633.3 17.4 %collective-permute-start.6 = (bf16[512,2048]{1,0:T(8,128)(2,1)S(1)}, bf16[512,2048]{1,0:T(8,128)(2,1)}, u32[]{:S(2)}, u32[]{:S(2)}) collective-permute-start(bf16[512,2048]{1,0:T(8,128)(2,1)S(1)} %copy-done.1), channel_id=1, source_target_pairs={{0,2},{2,0},{4,6},{6,4},{1,3},{3,1},{5,7},{7,5},{8,10},{10,8},{12,... | collective-permute-start | bytes 6291464 | tf_op jit(solution)/shard_map/ppermute | solution.py:292
  633.3 17.3 %collective-permute-start.7 = (bf16[512,2048]{1,0:T(8,128)(2,1)}, bf16[512,2048]{1,0:T(8,128)(2,1)}, u32[]{:S(2)}, u32[]{:S(2)}) collective-permute-start(bf16[512,2048]{1,0:T(8,128)(2,1)} %collective-permute-done.2.refs_1_), channel_id=1, source_target_pairs={{0,2},{2,0},{4,6},{6,4},{1,3},{3,1},{5,7},{7,5},{8,10},{10,8},{12,... | collective-permute-start | bytes 6291464 | tf_op jit(solution)/shard_map/ppermute | solution.py:292
  633.8 8.3 %collective-permute-start.4 = (bf16[1024,512]{1,0:T(8,128)(2,1)}, bf16[1024,512]{1,0:T(8,128)(2,1)}, u32[]{:S(2)}, u32[]{:S(2)}) collective-permute-start(bf16[1024,512]{1,0:T(8,128)(2,1)} %reduce-scatter.4.cloned.1.call-done.refs_0_), channel_id=1, source_target_pairs={{0,2},{2,0},{4,6},{6,4},{1,3},{3,1},{5,7},{7,5},{8,10},{10,8},{12,... | collective-permute-start | bytes 3145736 | tf_op jit(solution)/shard_map/ppermute | solution.py:292
  633.9 9.7 %collective-permute-start.5 = (bf16[1024,512]{1,0:T(8,128)(2,1)}, bf16[1024,512]{1,0:T(8,128)(2,1)}, u32[]{:S(2)}, u32[]{:S(2)}) collective-permute-start(bf16[1024,512]{1,0:T(8,128)(2,1)} %copy-done.4), channel_id=1, source_target_pairs={{0,2},{2,0},{4,6},{6,4},{1,3},{3,1},{5,7},{7,5},{8,10},{10,8},{12,... | collective-permute-start | bytes 3145736 | tf_op jit(solution)/shard_map/ppermute | solution.py:292
  634.3 26.7 %collective-permute-start.8 = (bf16[512,1024]{1,0:T(8,128)(2,1)}, bf16[512,1024]{1,0:T(8,128)(2,1)}, u32[]{:S(2)}, u32[]{:S(2)}) collective-permute-start(bf16[512,1024]{1,0:T(8,128)(2,1)} %reduce-scatter.8.cloned.1.call-done.refs_0_), channel_id=1, source_target_pairs={{0,4},{2,6},{4,0},{6,2},{1,5},{3,7},{5,1},{7,3},{8,12},{10,14},{12... | collective-permute-start | bytes 3145736 | tf_op jit(solution)/shard_map/ppermute | solution.py:292
  642.1 26.1 %collective-permute-start = (bf16[256,2048]{1,0:T(8,128)(2,1)S(1)}, bf16[256,2048]{1,0:T(8,128)(2,1)}, u32[]{:S(2)}, u32[]{:S(2)}) collective-permute-start(bf16[256,2048]{1,0:T(8,128)(2,1)S(1)} %copy-done.2), channel_id=1, source_target_pairs={{0,1},{1,0},{2,3},{3,2},{4,5},{5,4},{6,7},{7,6},{8,9},{9,8},{10,11... | collective-permute-start | bytes 3145736 | tf_op jit(solution)/shard_map/ppermute | solution.py:292
  650.1 39.8 %collective-permute-start.3 = (bf16[256,2048]{1,0:T(8,128)(2,1)}, bf16[256,2048]{1,0:T(8,128)(2,1)}, u32[]{:S(2)}, u32[]{:S(2)}) collective-permute-start(bf16[256,2048]{1,0:T(8,128)(2,1)} %get-tuple-element.92.refs_2_), channel_id=1, source_target_pairs={{0,1},{1,0},{2,3},{3,2},{4,5},{5,4},{6,7},{7,6},{8,9},{9,8},{10,11... | collective-permute-start | bytes 3145736 | tf_op jit(solution)/shard_map/ppermute | solution.py:292
  650.6 10.5 %copy-start.3 = (bf16[512,1024]{1,0:T(8,128)(2,1)S(1)}, bf16[512,1024]{1,0:T(8,128)(2,1)}, u32[]{:S(2)}) copy-start(bf16[512,1024]{1,0:T(8,128)(2,1)} %reduce-scatter.8.cloned.1.call-done.refs_0_) | copy-start | bytes 3145732
  661.1 33.8 %collective-permute-start.10 = (bf16[512,1024]{1,0:T(8,128)(2,1)}, bf16[512,1024]{1,0:T(8,128)(2,1)S(1)}, u32[]{:S(2)}, u32[]{:S(2)}) collective-permute-start(bf16[512,1024]{1,0:T(8,128)(2,1)} %collective-permute-done.8.refs_1_), channel_id=1, source_target_pairs={{0,2},{2,0},{4,6},{6,4},{1,3},{3,1},{5,7},{7,5},{8,10},{10,8},{12,... | collective-permute-start | bytes 3145736 | tf_op jit(solution)/shard_map/ppermute | solution.py:292
  661.1 33.8 %collective-permute-start.9 = (bf16[512,1024]{1,0:T(8,128)(2,1)S(1)}, bf16[512,1024]{1,0:T(8,128)(2,1)}, u32[]{:S(2)}, u32[]{:S(2)}) collective-permute-start(bf16[512,1024]{1,0:T(8,128)(2,1)S(1)} %copy-done.3), channel_id=1, source_target_pairs={{0,2},{2,0},{4,6},{6,4},{1,3},{3,1},{5,7},{7,5},{8,10},{10,8},{12,... | collective-permute-start | bytes 3145736 | tf_op jit(solution)/shard_map/ppermute | solution.py:292
  694.9 1.0 copy-start.5
Sparse Core Ops, SparseCore 0:
  10.1 83.5 all-gather.3
  95.9 148.1 all-gather.5
  245.7 78.9 all-gather.7
  326.8 75.3 reduce-scatter.3
  404.9 145.1 reduce-scatter.5
  552.8 77.4 reduce-scatter.7
